TPU v7x, 128 devices: a whole 4x4x4 slice. The times are simulated.
128 devices in a mesh: blk: 64 (over z, y_lo, x, core), dp: 2 (over y_hi).
Axes of the slice: x: 4, y: 4 (y_hi: 2, y_lo: 2; y = y_hi * 2 + y_lo), z: 4, core: 2. Of those that a mesh axis runs over, the one named last changes fastest.
Arguments:
- inputs: bfloat16 [16384, 1024], P(('blk', 'dp')), may hold values from -6 to 6
- cotangent: bfloat16 [16384, 1024], P(('blk', 'dp')), may hold values from -2.5 to 2.5
- task_ids: int32 [16384], P(('blk', 'dp')), may hold values from 0 to 3
- group_counts: int32 [128, 8], P(('blk', 'dp')), may hold values from 1 to 16, as said below
- task_gate: float32 [4, 64], replicated, may hold values from 0.25 to 2
- w_in: bfloat16 [64, 1024, 2048], P('blk'), may hold values from -0.1875 to 0.1875
- w_out: bfloat16 [64, 2048, 1024], P('blk'), may hold values from -0.125 to 0.125
Outputs:
- input_grad: float32 [16384, 1024], P(('blk', 'dp'))
- grad_in: float32 [64, 1024, 2048], P('blk', 'dp')
- grad_out: float32 [64, 2048, 1024], P('blk', 'dp')
Inputs may be any that keep to these rules, and one draw needn't show every extreme that they name: `group_counts`: in every draw one group has all 16 slots live on every device; the others vary from device to device.
All inputs are finite; a program needn't handle non-finite values.
Results may differ from a plain program's by a relative error of at most 0.0042.
Values may be sent and summed in bfloat16 or wider, within the bound.
A program may use at most 128 MiB of HBM per device.

v0:
```python
import jax
import jax.numpy as jnp
from jax import lax
from jax.sharding import PartitionSpec as P

grad_scale = 0.0625


def copy_for_each(array, axis):
    copies = jnp.broadcast_to(array, (lax.axis_size(axis), *array.shape))
    return lax.all_to_all(copies, axis, split_axis=0, concat_axis=0, tiled=True)


def laid_out(blocks, dim):
    shape = list(blocks.shape[1:])
    shape[dim] *= blocks.shape[0]
    return jnp.moveaxis(blocks, 0, dim).reshape(shape)


def gather_directly(array, axis, dim):
    blocks = copy_for_each(array, axis)
    return laid_out(blocks, dim)


def side_by_side(arrays, axis, dim, along):
    widths = [a.shape[along] for a in arrays]
    both = jnp.concatenate(arrays, axis=along)
    result = gather_directly(both, axis, dim)
    return tuple(jnp.split(result, [sum(widths[:k]) for k in range(1, len(widths))], axis=along))


def shortened(array):

    def short(part):
        return part.astype(jnp.bfloat16) if part.dtype == jnp.float32 else part

    return jax.tree.map(short, array)


def sent_together(arrays, axis, split_dim, concat_dim, along):
    widths = [a.shape[along] for a in arrays]
    both = jnp.concatenate(arrays, axis=along)
    result = lax.all_to_all(both, axis, split_axis=split_dim, concat_axis=concat_dim, tiled=True)
    return tuple(jnp.split(result, [sum(widths[:k]) for k in range(1, len(widths))], axis=along))


def silu_parts(pre_act):
    sigmoid_act = jax.nn.sigmoid(pre_act)
    return (pre_act * sigmoid_act, sigmoid_act * (1.0 + pre_act * (1.0 - sigmoid_act)))


def block_grads(x_rows, cot_rows, tag_rows, first_weight, second_weight, gate_column, cut):
    task_count = gate_column.shape[0]
    matches = tag_rows[:, None] == jnp.arange(task_count, dtype=jnp.int32)[None, :]
    row_gate = jnp.sum(jnp.where(matches, gate_column[None, :], 0.0), axis=1)
    pre_act = jnp.dot(x_rows, first_weight, preferred_element_type=jnp.float32)
    act_value, act_slope = silu_parts(pre_act)
    hidden = act_value.astype(jnp.bfloat16)
    scaled_cot = (row_gate[:, None] * cot_rows.astype(jnp.float32)).astype(jnp.bfloat16)
    hidden_cot = lax.dot_general(
        scaled_cot, second_weight, (((1,), (1,)), ((), ())), preferred_element_type=jnp.float32
    )
    pre_cot = (hidden_cot * act_slope).astype(jnp.bfloat16)
    part_index, part_count = cut
    first_span = x_rows.shape[1] // part_count
    second_span = hidden.shape[1] // part_count
    left_first = lax.dynamic_slice_in_dim(x_rows, part_index * first_span, first_span, 1)
    left_second = lax.dynamic_slice_in_dim(hidden, part_index * second_span, second_span, 1)
    grad_second = lax.dot_general(
        left_second, scaled_cot, (((0,), (0,)), ((), ())), preferred_element_type=jnp.float32
    )
    grad_first = lax.dot_general(
        left_first, pre_cot, (((0,), (0,)), ((), ())), preferred_element_type=jnp.float32
    )
    return (grad_first, grad_second, pre_cot)


def expert_rows(x_rows, cot_rows, tag_rows, first_weight, second_weight, gate_column, cut):
    row_count, model_width = x_rows.shape
    hidden_width = first_weight.shape[1]
    block_rows = min(512, row_count)
    first_rows, second_rows = (model_width // cut[1], hidden_width // cut[1])
    zero_first = jnp.zeros((first_rows, hidden_width), jnp.float32)
    zero_second = jnp.zeros((second_rows, model_width), jnp.float32)
    count_blocks = row_count // block_rows

    def step_block(carry, pieces):
        grad_first, grad_second, pre_cot = block_grads(
            pieces[0], pieces[1], pieces[2], first_weight, second_weight, gate_column, cut
        )
        return ((carry[0] + grad_first, carry[1] + grad_second), pre_cot)

    blocks_in = (
        x_rows.reshape(count_blocks, block_rows, model_width),
        cot_rows.reshape(count_blocks, block_rows, model_width),
        tag_rows.reshape(count_blocks, block_rows),
    )
    sums, pre_cots = lax.scan(step_block, (zero_first, zero_second), blocks_in)
    return (sums[0], sums[1], pre_cots.reshape(row_count, hidden_width))


def run_expert(x_rows, cot_rows, tag_rows, first_weight, second_weight, gate_column):
    row_count = x_rows.shape[0]
    both_x, both_cot, both_tags = (
        *side_by_side((x_rows, cot_rows), "dp", 0, 1),
        gather_directly(shortened(tag_rows), "dp", 0).astype(tag_rows.dtype),
    )
    half_index = lax.axis_index("dp")
    grad_first, grad_second, pre_cots = expert_rows(
        both_x,
        both_cot,
        both_tags,
        first_weight,
        second_weight,
        gate_column,
        (half_index, lax.axis_size("dp")),
    )
    own_pre = lax.dynamic_slice_in_dim(pre_cots, half_index * row_count, row_count, 0)
    row_grads = lax.dot_general(
        own_pre, first_weight, (((1,), (1,)), ((), ())), preferred_element_type=jnp.float32
    )
    return (grad_first, grad_second, row_grads)


def on_device(inputs, cotangent, task_ids, group_counts, task_gate, w_in, w_out):
    groups = group_counts.shape[1]
    model_width = inputs.shape[1]
    capacity = inputs.shape[0] // groups
    task_count = task_gate.shape[0]
    expert_count = lax.axis_size("blk")
    expert_index = lax.axis_index("blk")
    first_weight = w_in[0]
    second_weight = w_out[0]
    expert_match = jnp.arange(task_gate.shape[1], dtype=jnp.int32) == expert_index
    gate_column = jnp.sum(jnp.where(expert_match[None, :], task_gate, 0.0), axis=1)
    slot_index = jnp.arange(capacity, dtype=jnp.int32)
    live_slots = slot_index[None, :] < group_counts[0][:, None]
    seg_tags = jnp.where(live_slots, task_ids.reshape(groups, capacity), task_count)
    seg_x = inputs.reshape(groups, capacity, model_width)
    seg_cot = cotangent.reshape(groups, capacity, model_width)
    repeats = expert_count // groups
    send_x = jnp.broadcast_to(seg_x[None], (repeats, groups, capacity, model_width)).reshape(
        expert_count, capacity, model_width
    )
    send_cot = jnp.broadcast_to(seg_cot[None], (repeats, groups, capacity, model_width)).reshape(
        expert_count, capacity, model_width
    )
    send_tags = jnp.broadcast_to(seg_tags[None], (repeats, groups, capacity)).reshape(
        expert_count, capacity
    )
    recv_x, recv_cot, recv_tags = (
        *sent_together((send_x, send_cot), "blk", 0, 0, 1),
        lax.all_to_all(send_tags, "blk", split_axis=0, concat_axis=0, tiled=True),
    )
    grad_first, grad_second, row_grads = run_expert(
        recv_x.reshape(expert_count * capacity, model_width),
        recv_cot.reshape(expert_count * capacity, model_width),
        recv_tags.reshape(expert_count * capacity),
        first_weight,
        second_weight,
        gate_column,
    )
    returned = lax.all_to_all(
        row_grads.reshape(expert_count, capacity, model_width).astype(jnp.bfloat16),
        "blk",
        split_axis=0,
        concat_axis=0,
        tiled=True,
    ).astype(jnp.float32)
    input_home = jnp.sum(returned.reshape(repeats, groups, capacity, model_width), axis=0)
    first_out = (grad_first * grad_scale)[None]
    second_out = (grad_second * grad_scale)[None]
    return (input_home.reshape(groups * capacity, model_width), first_out, second_out)


def solution(mesh):
    in_specs = (
        P(("blk", "dp"), None),
        P(("blk", "dp"), None),
        P(("blk", "dp")),
        P(("blk", "dp"), None),
        P(),
        P("blk", None, None),
        P("blk", None, None),
    )
    out_specs = (P(("blk", "dp"), None), P("blk", "dp", None), P("blk", "dp", None))
    return jax.shard_map(
        on_device, mesh=mesh, in_specs=in_specs, out_specs=out_specs, check_vma=False
    )
```

profile of v0, /device:TPU:1, one launch (start us, length us, event | category | flops | bytes accessed | tf_op | source)
XLA Modules:
  0.0 320.6 jit_solution(16967445388201600989)
XLA Ops:
  0.6 0.7 reshape.106
  1.4 0.7 fusion.19
  2.1 0.6 broadcast_in_dim.102
  2.7 10.8 %all-to-all-start.2 = ((s32[64,1,16]{2,1,0:T(1,128)}), s32[64,1,16]{2,1,0:T(1,128)S(1)}, u32[]{:S(2)}, u32[]{:S(2)}) async-start(s32[64,1,16]{2,1,0:T(1,128)} %bitcast.9), calls=%async_computation.2 | async-start | bytes 65536 | tf_op jit(solution)/shard_map/all_to_all | solution.py:153
  13.6 1.2 broadcast_in_dim.97
  14.8 1.2 broadcast_in_dim.99
  16.0 2.8 pad_maximum_fusion
  18.8 2.5 all-to-all-done.2
  21.3 6.6 %all-to-all-start = ((bf16[64,32,1024]{2,1,0:T(8,128)(2,1)}), bf16[64,32,1024]{2,1,0:T(8,128)(2,1)}, u32[]{:S(2)}, u32[]{:S(2)}) async-start(bf16[64,32,1024]{2,1,0:T(8,128)(2,1)} %pad_maximum_fusion), calls=%async_computation | async-start | bytes 8388608 | tf_op jit(solution)/shard_map/all_to_all | solution.py:43
  28.4 0.7 reduce.4
  29.2 50.6 %all-to-all-done = bf16[64,32,1024]{2,1,0:T(8,128)(2,1)} async-done(((bf16[64,32,1024]{2,1,0:T(8,128)(2,1)}), bf16[64,32,1024]{2,1,0:T(8,128)(2,1)}, u32[]{:S(2)}, u32[]{:S(2)}) %all-to-all-start) | async-done | bytes 4194336 | tf_op jit(solution)/shard_map/all_to_all | solution.py:43
  79.8 0.6 broadcast_in_dim.104
  80.4 3.9 %all-to-all-start.3 = ((s32[2,1,1024]{2,1,0:T(1,128)}), s32[2,1,1024]{2,1,0:T(1,128)S(1)}, u32[]{:S(2)}, u32[]{:S(2)}) async-start(s32[2,1,1024]{2,1,0:T(1,128)} %broadcast_in_dim.104), calls=%async_computation.3 | async-start | bytes 16384 | tf_op jit(solution)/shard_map/all_to_all | solution.py:11
  84.3 3.1 fusion.21
  87.4 2.5 pad_maximum_fusion.1
  89.8 6.8 %broadcast_in_dim.100 = bf16[2,1024,2048]{2,1,0:T(8,128)(2,1)} broadcast(bf16[1024,2048]{1,0:T(8,128)(2,1)} %pad_maximum_fusion.1), dimensions={1,2} | broadcast | bytes 12582912 | tf_op jit(solution)/shard_map/broadcast_in_dim | solution.py:10
  96.6 7.3 %all-to-all-start.1 = ((bf16[2,1024,2048]{2,1,0:T(8,128)(2,1)}), bf16[2,1024,2048]{2,1,0:T(8,128)(2,1)}, u32[]{:S(2)}, u32[]{:S(2)}) async-start(bf16[2,1024,2048]{2,1,0:T(8,128)(2,1)} %broadcast_in_dim.100), calls=%async_computation.1 | async-start | bytes 16777216 | tf_op jit(solution)/shard_map/all_to_all | solution.py:11
  104.1 93.7 %all-to-all-done.1 = bf16[2,1024,2048]{2,1,0:T(8,128)(2,1)} async-done(((bf16[2,1024,2048]{2,1,0:T(8,128)(2,1)}), bf16[2,1024,2048]{2,1,0:T(8,128)(2,1)}, u32[]{:S(2)}, u32[]{:S(2)}) %all-to-all-start.1) | async-done | bytes 8388640 | tf_op jit(solution)/shard_map/all_to_all | solution.py:11
  197.8 5.9 %fusion.20 = (bf16[2048,1024]{1,0:T(8,128)(2,1)}, bf16[2048,1024]{1,0:T(8,128)(2,1)}) fusion(bf16[2048,2048]{1,0:T(8,128)(2,1)} %bitcast.6), kind=kLoop, calls=%fused_computation.34 | loop fusion | bytes 16777216 | tf_op jit(solution)/shard_map/split | solution.py:29
  203.8 69.1 %while.18 = (s32[]{:T(128)}, f32[512,2048]{1,0:T(8,128)}, f32[1024,1024]{1,0:T(8,128)}, bf16[4,512,2048]{2,1,0:T(8,128)(2,1)}, bf16[4,512,1024]{2,1,0:T(8,128)(2...) while((s32[]{:T(128)}, f32[512,2048]{1,0:T(8,128)}, ...), condition=%wide.region_3.4_spmd.clone, body=%wide.region_1.3_spmd.clone.sunk | while | flops 6463428096 | bytes 152582032 | solution.py:98
  203.9 5.4 %add_divide_fusion.2 = (f32[512,2048]{1,0:T(8,128)S(1)}, f32[512,2048]{1,0:T(8,128)S(1)}) fusion(bf16[1024,2048]{1,0:T(8,128)(2,1)} %get-tuple-element.400, bf16[4,512,1024]{2,1,0:T(8,128)(2,1)} %get-tuple-element.394, s32[]{:T(128)S(6)} %copy.15), kind=kOutput, calls=%fused_computation.3.clone.2 | convolution fusion | flops 2150629376 | bytes 13631492 | tf_op jit(solution)/shard_map/while/body/eval_jaxpr/dot_general | solution.py:56
  209.3 2.1 select_add_fusion.5
  211.5 4.4 %bitcast_dynamic-update-slice_fusion.2 = (bf16[4,512,2048]{2,1,0:T(8,128)(2,1)}, bf16[512,2048]{1,0:T(8,128)(2,1)S(1)}) fusion(bf16[4,512,2048]{2,1,0:T(8,128)(2,1)} %get-tuple-element.378, s32[]{:T(128)S(6)} %copy.15, f32[512,2048]{1,0:T(8,128)S(1)} %get-tuple-element.356, bf16[2048,1024]{1,0:T(8,128)(2,1)S(1)} %copy-done.7, ...), kind=kOutput, calls=%fused_computation.8.clone.1 | convolution fusion | flops 2158493696 | bytes 13634560 | tf_op jit(solution)/shard_map/while/body/eval_jaxpr/dot_general | solution.py:60
  215.9 3.1 select_add_fusion.4
  219.1 2.0 copy-done.3
  221.2 5.4 %add_divide_fusion.2 = (f32[512,2048]{1,0:T(8,128)S(1)}, f32[512,2048]{1,0:T(8,128)S(1)}) fusion(bf16[1024,2048]{1,0:T(8,128)(2,1)} %get-tuple-element.400, bf16[4,512,1024]{2,1,0:T(8,128)(2,1)} %get-tuple-element.394, s32[]{:T(128)S(6)} %copy.15), kind=kOutput, calls=%fused_computation.3.clone.2 | convolution fusion | flops 2150629376 | bytes 13631492 | tf_op jit(solution)/shard_map/while/body/eval_jaxpr/dot_general | solution.py:56
  226.6 2.1 select_add_fusion.5
  228.8 4.4 %bitcast_dynamic-update-slice_fusion.2 = (bf16[4,512,2048]{2,1,0:T(8,128)(2,1)}, bf16[512,2048]{1,0:T(8,128)(2,1)S(1)}) fusion(bf16[4,512,2048]{2,1,0:T(8,128)(2,1)} %get-tuple-element.378, s32[]{:T(128)S(6)} %copy.15, f32[512,2048]{1,0:T(8,128)S(1)} %get-tuple-element.356, bf16[2048,1024]{1,0:T(8,128)(2,1)S(1)} %copy-done.7, ...), kind=kOutput, calls=%fused_computation.8.clone.1 | convolution fusion | flops 2158493696 | bytes 13634560 | tf_op jit(solution)/shard_map/while/body/eval_jaxpr/dot_general | solution.py:60
  233.2 3.1 select_add_fusion.4
  236.3 2.0 copy-done.3
  238.4 5.4 %add_divide_fusion.2 = (f32[512,2048]{1,0:T(8,128)S(1)}, f32[512,2048]{1,0:T(8,128)S(1)}) fusion(bf16[1024,2048]{1,0:T(8,128)(2,1)} %get-tuple-element.400, bf16[4,512,1024]{2,1,0:T(8,128)(2,1)} %get-tuple-element.394, s32[]{:T(128)S(6)} %copy.15), kind=kOutput, calls=%fused_computation.3.clone.2 | convolution fusion | flops 2150629376 | bytes 13631492 | tf_op jit(solution)/shard_map/while/body/eval_jaxpr/dot_general | solution.py:56
  243.9 2.1 select_add_fusion.5
  246.1 4.4 %bitcast_dynamic-update-slice_fusion.2 = (bf16[4,512,2048]{2,1,0:T(8,128)(2,1)}, bf16[512,2048]{1,0:T(8,128)(2,1)S(1)}) fusion(bf16[4,512,2048]{2,1,0:T(8,128)(2,1)} %get-tuple-element.378, s32[]{:T(128)S(6)} %copy.15, f32[512,2048]{1,0:T(8,128)S(1)} %get-tuple-element.356, bf16[2048,1024]{1,0:T(8,128)(2,1)S(1)} %copy-done.7, ...), kind=kOutput, calls=%fused_computation.8.clone.1 | convolution fusion | flops 2158493696 | bytes 13634560 | tf_op jit(solution)/shard_map/while/body/eval_jaxpr/dot_general | solution.py:60
  250.5 3.1 select_add_fusion.4
  253.6 2.0 copy-done.3
  255.7 5.4 %add_divide_fusion.2 = (f32[512,2048]{1,0:T(8,128)S(1)}, f32[512,2048]{1,0:T(8,128)S(1)}) fusion(bf16[1024,2048]{1,0:T(8,128)(2,1)} %get-tuple-element.400, bf16[4,512,1024]{2,1,0:T(8,128)(2,1)} %get-tuple-element.394, s32[]{:T(128)S(6)} %copy.15), kind=kOutput, calls=%fused_computation.3.clone.2 | convolution fusion | flops 2150629376 | bytes 13631492 | tf_op jit(solution)/shard_map/while/body/eval_jaxpr/dot_general | solution.py:56
  261.2 2.1 select_add_fusion.5
  263.4 4.4 %bitcast_dynamic-update-slice_fusion.2 = (bf16[4,512,2048]{2,1,0:T(8,128)(2,1)}, bf16[512,2048]{1,0:T(8,128)(2,1)S(1)}) fusion(bf16[4,512,2048]{2,1,0:T(8,128)(2,1)} %get-tuple-element.378, s32[]{:T(128)S(6)} %copy.15, f32[512,2048]{1,0:T(8,128)S(1)} %get-tuple-element.356, bf16[2048,1024]{1,0:T(8,128)(2,1)S(1)} %copy-done.7, ...), kind=kOutput, calls=%fused_computation.8.clone.1 | convolution fusion | flops 2158493696 | bytes 13634560 | tf_op jit(solution)/shard_map/while/body/eval_jaxpr/dot_general | solution.py:60
  267.8 3.1 select_add_fusion.4
  270.9 2.0 copy-done.3
  272.9 2.7 constant_dynamic-slice_fusion.1
  275.5 0.8 copy-done.8
  276.3 5.8 %fusion.16 = bf16[64,16,1024]{2,1,0:T(8,128)(2,1)} fusion(bf16[64,16,2048]{2,1,0:T(8,128)(2,1)S(1)} %bitcast.74, bf16[1,1024,2048]{2,1,0:T(8,128)(2,1)S(1)} %bitcast.83), kind=kOutput, calls=%fused_computation.28 | convolution fusion | flops 4296015872 | bytes 10485760 | tf_op jit(solution)/shard_map/dot_general | solution.py:119
  282.1 8.0 %all-to-all-start.4 = ((bf16[64,16,1024]{2,1,0:T(8,128)(2,1)}), bf16[64,16,1024]{2,1,0:T(8,128)(2,1)S(1)}, u32[]{:S(2)}, u32[]{:S(2)}) async-start(bf16[64,16,1024]{2,1,0:T(8,128)(2,1)} %fusion.16), calls=%async_computation.4 | async-start | bytes 4194304 | tf_op jit(solution)/shard_map/all_to_all | solution.py:163
  290.2 5.2 %multiply_bitcast_fusion = f32[1,1024,1024]{2,1,0:T(8,128)} fusion(f32[1024,1024]{1,0:T(8,128)} %get-tuple-element.207), kind=kLoop, calls=%fused_computation.26 | loop fusion | flops 1048576 | bytes 8388608 | tf_op jit(solution)/shard_map/broadcast_in_dim | solution.py:172
  295.4 2.3 multiply_bitcast_fusion.1
  297.7 21.8 %all-to-all-done.4 = bf16[64,16,1024]{2,1,0:T(8,128)(2,1)S(1)} async-done(((bf16[64,16,1024]{2,1,0:T(8,128)(2,1)}), bf16[64,16,1024]{2,1,0:T(8,128)(2,1)S(1)}, u32[]{:S(2)}, u32[]{:S(2)}) %all-to-all-start.4) | async-done | bytes 2097184 | tf_op jit(solution)/shard_map/all_to_all | solution.py:163
  319.5 1.1 convert_reduce_fusion
  (67 shorter events, 1.6 us)
Async XLA Ops:
  2.7 18.6 %all-to-all-start.2 = ((s32[64,1,16]{2,1,0:T(1,128)}), s32[64,1,16]{2,1,0:T(1,128)S(1)}, u32[]{:S(2)}, u32[]{:S(2)}) async-start(s32[64,1,16]{2,1,0:T(1,128)} %bitcast.9), calls=%async_computation.2 | async-start | bytes 65536 | tf_op jit(solution)/shard_map/all_to_all | solution.py:153
  21.3 58.5 %all-to-all-start = ((bf16[64,32,1024]{2,1,0:T(8,128)(2,1)}), bf16[64,32,1024]{2,1,0:T(8,128)(2,1)}, u32[]{:S(2)}, u32[]{:S(2)}) async-start(bf16[64,32,1024]{2,1,0:T(8,128)(2,1)} %pad_maximum_fusion), calls=%async_computation | async-start | bytes 8388608 | tf_op jit(solution)/shard_map/all_to_all | solution.py:43
  80.4 9.4 %all-to-all-start.3 = ((s32[2,1,1024]{2,1,0:T(1,128)}), s32[2,1,1024]{2,1,0:T(1,128)S(1)}, u32[]{:S(2)}, u32[]{:S(2)}) async-start(s32[2,1,1024]{2,1,0:T(1,128)} %broadcast_in_dim.104), calls=%async_computation.3 | async-start | bytes 16384 | tf_op jit(solution)/shard_map/all_to_all | solution.py:11
  96.6 7.3 %copy-start.6 = (f32[4,64]{1,0:T(4,128)S(1)}, f32[4,64]{1,0:T(4,128)}, u32[]{:S(2)}) copy-start(f32[4,64]{1,0:T(4,128)} %param.13) | copy-start | bytes 3076
  96.6 101.3 %all-to-all-start.1 = ((bf16[2,1024,2048]{2,1,0:T(8,128)(2,1)}), bf16[2,1024,2048]{2,1,0:T(8,128)(2,1)}, u32[]{:S(2)}, u32[]{:S(2)}) async-start(bf16[2,1024,2048]{2,1,0:T(8,128)(2,1)} %broadcast_in_dim.100), calls=%async_computation.1 | async-start | bytes 16777216 | tf_op jit(solution)/shard_map/all_to_all | solution.py:11
  203.9 5.5 %copy-start = (f32[1024,1024]{1,0:T(8,128)S(1)}, f32[1024,1024]{1,0:T(8,128)}, u32[]{:S(2)}) copy-start(f32[1024,1024]{1,0:T(8,128)} %get-tuple-element.377) | copy-start | bytes 12582916 | tf_op jit(solution)/shard_map/while
  203.9 5.5 %copy-start.5 = (bf16[4,512,1024]{2,1,0:T(8,128)(2,1)S(1)}, bf16[4,512,1024]{2,1,0:T(8,128)(2,1)}, u32[]{:S(2)}) copy-start(bf16[4,512,1024]{2,1,0:T(8,128)(2,1)} %get-tuple-element.398) | copy-start | bytes 12582916 | tf_op jit(solution)/shard_map/while
  209.3 2.2 copy-start.7
  211.5 4.4 %copy-start.1 = (f32[1024,1024]{1,0:T(8,128)}, f32[1024,1024]{1,0:T(8,128)S(1)}, u32[]{:S(2)}) copy-start(f32[1024,1024]{1,0:T(8,128)S(1)} %select_add_fusion.5) | copy-start | bytes 12582916 | tf_op jit(solution)/shard_map/while
  211.5 4.4 %copy-start.2 = (f32[512,2048]{1,0:T(8,128)S(1)}, f32[512,2048]{1,0:T(8,128)}, u32[]{:S(2)}) copy-start(f32[512,2048]{1,0:T(8,128)} %get-tuple-element.376) | copy-start | bytes 12582916 | tf_op jit(solution)/shard_map/while
  219.1 2.0 copy-start.3
  221.2 5.4 %copy-start = (f32[1024,1024]{1,0:T(8,128)S(1)}, f32[1024,1024]{1,0:T(8,128)}, u32[]{:S(2)}) copy-start(f32[1024,1024]{1,0:T(8,128)} %get-tuple-element.377) | copy-start | bytes 12582916 | tf_op jit(solution)/shard_map/while
  221.2 5.5 %copy-start.5 = (bf16[4,512,1024]{2,1,0:T(8,128)(2,1)S(1)}, bf16[4,512,1024]{2,1,0:T(8,128)(2,1)}, u32[]{:S(2)}) copy-start(bf16[4,512,1024]{2,1,0:T(8,128)(2,1)} %get-tuple-element.398) | copy-start | bytes 12582916 | tf_op jit(solution)/shard_map/while
  226.6 2.2 copy-start.7
  228.8 4.4 %copy-start.1 = (f32[1024,1024]{1,0:T(8,128)}, f32[1024,1024]{1,0:T(8,128)S(1)}, u32[]{:S(2)}) copy-start(f32[1024,1024]{1,0:T(8,128)S(1)} %select_add_fusion.5) | copy-start | bytes 12582916 | tf_op jit(solution)/shard_map/while
  228.8 4.4 %copy-start.2 = (f32[512,2048]{1,0:T(8,128)S(1)}, f32[512,2048]{1,0:T(8,128)}, u32[]{:S(2)}) copy-start(f32[512,2048]{1,0:T(8,128)} %get-tuple-element.376) | copy-start | bytes 12582916 | tf_op jit(solution)/shard_map/while
  236.3 2.0 copy-start.3
  238.4 5.4 %copy-start = (f32[1024,1024]{1,0:T(8,128)S(1)}, f32[1024,1024]{1,0:T(8,128)}, u32[]{:S(2)}) copy-start(f32[1024,1024]{1,0:T(8,128)} %get-tuple-element.377) | copy-start | bytes 12582916 | tf_op jit(solution)/shard_map/while
  238.4 5.5 %copy-start.5 = (bf16[4,512,1024]{2,1,0:T(8,128)(2,1)S(1)}, bf16[4,512,1024]{2,1,0:T(8,128)(2,1)}, u32[]{:S(2)}) copy-start(bf16[4,512,1024]{2,1,0:T(8,128)(2,1)} %get-tuple-element.398) | copy-start | bytes 12582916 | tf_op jit(solution)/shard_map/while
  243.9 2.2 copy-start.7
  246.1 4.4 %copy-start.1 = (f32[1024,1024]{1,0:T(8,128)}, f32[1024,1024]{1,0:T(8,128)S(1)}, u32[]{:S(2)}) copy-start(f32[1024,1024]{1,0:T(8,128)S(1)} %select_add_fusion.5) | copy-start | bytes 12582916 | tf_op jit(solution)/shard_map/while
  246.1 4.4 %copy-start.2 = (f32[512,2048]{1,0:T(8,128)S(1)}, f32[512,2048]{1,0:T(8,128)}, u32[]{:S(2)}) copy-start(f32[512,2048]{1,0:T(8,128)} %get-tuple-element.376) | copy-start | bytes 12582916 | tf_op jit(solution)/shard_map/while
  253.6 2.0 copy-start.3
  255.7 5.4 %copy-start = (f32[1024,1024]{1,0:T(8,128)S(1)}, f32[1024,1024]{1,0:T(8,128)}, u32[]{:S(2)}) copy-start(f32[1024,1024]{1,0:T(8,128)} %get-tuple-element.377) | copy-start | bytes 12582916 | tf_op jit(solution)/shard_map/while
  255.7 5.5 %copy-start.5 = (bf16[4,512,1024]{2,1,0:T(8,128)(2,1)S(1)}, bf16[4,512,1024]{2,1,0:T(8,128)(2,1)}, u32[]{:S(2)}) copy-start(bf16[4,512,1024]{2,1,0:T(8,128)(2,1)} %get-tuple-element.398) | copy-start | bytes 12582916 | tf_op jit(solution)/shard_map/while
  261.2 2.2 copy-start.7
  263.4 4.4 %copy-start.1 = (f32[1024,1024]{1,0:T(8,128)}, f32[1024,1024]{1,0:T(8,128)S(1)}, u32[]{:S(2)}) copy-start(f32[1024,1024]{1,0:T(8,128)S(1)} %select_add_fusion.5) | copy-start | bytes 12582916 | tf_op jit(solution)/shard_map/while
  263.4 4.4 %copy-start.2 = (f32[512,2048]{1,0:T(8,128)S(1)}, f32[512,2048]{1,0:T(8,128)}, u32[]{:S(2)}) copy-start(f32[512,2048]{1,0:T(8,128)} %get-tuple-element.376) | copy-start | bytes 12582916 | tf_op jit(solution)/shard_map/while
  270.9 2.0 copy-start.3
  272.9 3.4 %copy-start.8 = (bf16[1024,2048]{1,0:T(8,128)(2,1)S(1)}, bf16[1024,2048]{1,0:T(8,128)(2,1)}, u32[]{:S(2)}) copy-start(bf16[1024,2048]{1,0:T(8,128)(2,1)} %get-tuple-element.414) | copy-start | bytes 12582916
  282.1 37.3 %all-to-all-start.4 = ((bf16[64,16,1024]{2,1,0:T(8,128)(2,1)}), bf16[64,16,1024]{2,1,0:T(8,128)(2,1)S(1)}, u32[]{:S(2)}, u32[]{:S(2)}) async-start(bf16[64,16,1024]{2,1,0:T(8,128)(2,1)} %fusion.16), calls=%async_computation.4 | async-start | bytes 4194304 | tf_op jit(solution)/shard_map/all_to_all | solution.py:163
  290.1 5.2 %copy-start.4 = (f32[512,2048]{1,0:T(8,128)S(1)}, f32[512,2048]{1,0:T(8,128)}, u32[]{:S(2)}) copy-start(f32[512,2048]{1,0:T(8,128)} %get-tuple-element.206) | copy-start | bytes 12582916
where the time goes:
time: 322 us; the launch traced here: 321 us
  waiting for transfers between devices  169 us (52%)
  matrix products  65.9 us (20%)
  starting transfers between devices  36.5 us (11%)
  local copies, waits for them, and re-layouts  32.6 us (10%)
  other arithmetic  15.9 us (5%)
    all_to_all x2, waiting for transfers between devices, copy_for_each(): return lax.all_to_all(copies, axis, split_axis=0, concat_axis=0, tiled=True)  93.7 us
    all_to_all x1, waiting for transfers between devices, sent_together(): lax.all_to_all(both, axis, split_axis=split_dim, concat_axis=concat_dim,...  50.6 us
    all_to_all x1, waiting for transfers between devices, on_device(): lax.all_to_all(row_grads.reshape(expert_count, capacity, model_width).ast...  21.8 us
    dot_general x4, matrix products, block_grads(): pre_act = jnp.dot(x_rows, first_weight, preferred_element_type=jnp.float32)  21.7 us
    dot_general x4, matrix products, block_grads(): lax.dot_general(scaled_cot, second_weight, (((1,), (1,)), ((), ())), pref...  17.6 us
    dot_general x4, matrix products, block_grads(): lax.dot_general(left_first, pre_cot, (((0,), (0,)), ((), ())), preferred_...  12.4 us
    all_to_all x2, starting transfers between devices, copy_for_each(): return lax.all_to_all(copies, axis, split_axis=0, concat_axis=0, tiled=True)  11.2 us
    all_to_all x1, starting transfers between devices, on_device(): lax.all_to_all(send_tags, 'blk', split_axis=0, concat_axis=0, tiled=True)  10.8 us
  transfers between devices with their start and end apart: 5, of which 4 were waited for; matrix products, arithmetic and copies ran while one was open for 6% of the time, Pallas kernels for 0%

commit v1 on v0

v1 whole, which is shorter than its diff:
```python
import jax
import jax.numpy as jnp
import numpy as np
from jax import lax
from jax.sharding import Mesh, PartitionSpec as P

grad_scale = 0.0625
LINE = ("x", "core")
PLANE = ("z", "ylo", "yhi")


def silu_parts(pre_act):
    sig = jax.nn.sigmoid(pre_act)
    return pre_act * sig, sig * (1.0 + pre_act * (1.0 - sig))


def on_device(inputs, cotangent, task_ids, group_counts, task_gate, w_in, w_out):
    groups = group_counts.shape[1]
    width = inputs.shape[1]
    cap = inputs.shape[0] // groups
    tasks = task_gate.shape[0]
    expert = (lax.axis_index("z") * lax.axis_size("ylo") + lax.axis_index("ylo")) * groups + lax.axis_index(
        "x"
    ) * lax.axis_size("core") + lax.axis_index("core")
    half = lax.axis_index("yhi")
    w1, w2 = w_in[0], w_out[0]
    hidden = w1.shape[1]
    match = jnp.arange(task_gate.shape[1], dtype=jnp.int32) == expert
    gate_column = jnp.sum(jnp.where(match[None, :], task_gate, 0.0), axis=1)
    live = jnp.arange(cap, dtype=jnp.int32)[None, :] < group_counts[0][:, None]
    tags = jnp.where(live, task_ids.reshape(groups, cap), tasks)
    both = jnp.concatenate([inputs, cotangent], axis=1).reshape(groups, cap, 2 * width)
    both = lax.all_to_all(both, LINE, split_axis=0, concat_axis=0, tiled=True)
    tags = lax.all_to_all(tags, LINE, split_axis=0, concat_axis=0, tiled=True)
    rows = lax.all_gather(both.reshape(groups * cap, 2 * width), PLANE, axis=0, tiled=False)
    tags = lax.all_gather(tags.reshape(groups * cap), PLANE, axis=0, tiled=False)
    nodes = rows.shape[0]
    count = nodes * groups * cap
    own = groups * cap
    x = rows[:, :, :width].reshape(count, width)
    cot = rows[:, :, width:].reshape(count, width)
    tags = tags.reshape(count)
    gate = jnp.sum(
        jnp.where(tags[:, None] == jnp.arange(tasks, dtype=jnp.int32)[None, :], gate_column[None, :], 0.0), axis=1
    )
    pre = jnp.dot(x, w1, preferred_element_type=jnp.float32)
    act, slope = silu_parts(pre)
    act = act.astype(jnp.bfloat16)
    scaled = (gate[:, None] * cot.astype(jnp.float32)).astype(jnp.bfloat16)
    back = lax.dot_general(scaled, w2, (((1,), (1,)), ((), ())), preferred_element_type=jnp.float32)
    pre_grad = (back * slope).astype(jnp.bfloat16)
    left1 = lax.dynamic_slice_in_dim(x, half * (width // 2), width // 2, 1)
    left2 = lax.dynamic_slice_in_dim(act, half * (hidden // 2), hidden // 2, 1)
    grad_out = lax.dot_general(left2, scaled, (((0,), (0,)), ((), ())), preferred_element_type=jnp.float32)
    grad_in = lax.dot_general(left1, pre_grad, (((0,), (0,)), ((), ())), preferred_element_type=jnp.float32)
    own_pre = pre_grad.reshape(nodes // 2, 2, own, hidden)
    own_pre = lax.dynamic_index_in_dim(own_pre, half, 1, keepdims=False)
    row_grad = lax.dot_general(
        own_pre.reshape(nodes // 2 * own, hidden), w1, (((1,), (1,)), ((), ())), preferred_element_type=jnp.float32
    )
    row_grad = row_grad.reshape(nodes // 2, own, width).astype(jnp.bfloat16)
    row_grad = lax.all_to_all(row_grad, ("z", "ylo"), split_axis=0, concat_axis=0, tiled=True)
    row_grad = jnp.sum(row_grad.astype(jnp.float32), axis=0).astype(jnp.bfloat16)
    home = lax.all_to_all(row_grad.reshape(groups, cap, width), LINE, split_axis=0, concat_axis=0, tiled=True)
    return (
        home.astype(jnp.float32).reshape(groups * cap, width),
        (grad_in * grad_scale)[None],
        (grad_out * grad_scale)[None],
    )


def solution(mesh):
    fine = Mesh(mesh.devices.reshape(4, 2, 4, 2, 2), ("z", "ylo", "x", "core", "yhi"))
    blk = ("z", "ylo", "x", "core")
    every = blk + ("yhi",)
    in_specs = (P(every, None), P(every, None), P(every), P(every, None), P(), P(blk, None, None), P(blk, None, None))
    out_specs = (P(every, None), P(blk, "yhi", None), P(blk, "yhi", None))
    return jax.shard_map(on_device, mesh=fine, in_specs=in_specs, out_specs=out_specs, check_vma=False)
```

time: 322 us -> 316 us (0.981)
  blocking collectives: 0 us -> 55.3 us
  local copies, waits for them, and re-layouts: 32.6 us -> 1.34 us
  waiting for transfers between devices: 169 us -> 146 us
  starting transfers between devices: 36.5 us -> 14 us
  between operations: 0.78 us -> 14.1 us
    all_to_all x5 -> x3, waiting for transfers between devices: 169 us -> 14.3 us  [the longest x1 10.6 us: on_device(): lax.all_to_all(row_grad, ('z', 'ylo'), split_axis=0, concat_axis=0, tiled...]
    all_gather x0 -> x1, waiting for transfers between devices: none -> 132 us  [on_device(): lax.all_gather(both.reshape(groups * cap, 2 * width), PLANE, axis=0, tile...]
    all_gather x0 -> x1, blocking collectives: none -> 40.3 us  [on_device(): lax.all_gather(tags.reshape(groups * cap), PLANE, axis=0, tiled=False)]
    all_to_all x5 -> x3, starting transfers between devices: 36.5 us -> 13.9 us  [the longest x1 5.91 us: on_device(): lax.all_to_all(row_grad.reshape(groups, cap, width), LINE, split_axis=0,...]
    all_to_all x0 -> x1, blocking collectives: none -> 15 us  [on_device(): both = lax.all_to_all(both, LINE, split_axis=0, concat_axis=0, tiled=True)]
    convert_element_type x0 -> x3, other arithmetic: none -> 11.2 us  [on_device(): scaled = (gate[:, None] * cot.astype(jnp.float32)).astype(jnp.bfloat16)]
    broadcast_in_dim x6 -> x0, local copies, waits for them, and re-layouts: 10.5 us -> none  [the longest x3 7.44 us: copy_for_each(): copies = jnp.broadcast_to(array, (lax.axis_size(axis), *array.shape))]
    split x2 -> x0, local copies, waits for them, and re-layouts: 8.98 us -> none  [the longest x1 5.92 us: side_by_side(): jnp.split(result, [sum(widths[:k]) for k in range(1, len(widths))], axis=...]
  transfers between devices with their start and end apart: 5 -> 4, of which waited for: 4 -> 3; matrix products, arithmetic and copies ran while one was open for 6% -> 10% of each run, Pallas kernels for 0% -> 0%
where the time goes in v1:
time: 316 us; the launch traced here: 315 us
  waiting for transfers between devices  146 us (46%)
  matrix products  66.6 us (21%)
  blocking collectives  55.3 us (18%)
  other arithmetic  17.1 us (5%)
  between operations  14.1 us (4%)
  starting transfers between devices  14 us (4%)
    all_gather x1, waiting for transfers between devices, on_device(): lax.all_gather(both.reshape(groups * cap, 2 * width), PLANE, axis=0, tile...  132 us
    all_gather x1, blocking collectives, on_device(): lax.all_gather(tags.reshape(groups * cap), PLANE, axis=0, tiled=False)  40.3 us
    dot_general x1, matrix products, on_device(): pre = jnp.dot(x, w1, preferred_element_type=jnp.float32)  19.2 us
    dot_general x1, matrix products, on_device(): lax.dot_general(scaled, w2, (((1,), (1,)), ((), ())), preferred_element_t...  17.3 us
    all_to_all x1, blocking collectives, on_device(): both = lax.all_to_all(both, LINE, split_axis=0, concat_axis=0, tiled=True)  15 us
    dot_general x1, matrix products, on_device(): lax.dot_general(left2, scaled, (((0,), (0,)), ((), ())), preferred_elemen...  11.5 us
    convert_element_type x3, other arithmetic, on_device(): scaled = (gate[:, None] * cot.astype(jnp.float32)).astype(jnp.bfloat16)  11.2 us
    dot_general x1, matrix products, on_device(): lax.dot_general(left1, pre_grad, (((0,), (0,)), ((), ())), preferred_elem...  10.6 us
  transfers between devices with their start and end apart: 4, of which 3 were waited for; matrix products, arithmetic and copies ran while one was open for 10% of the time, Pallas kernels for 0%

profile of v1, /device:TPU:1, one launch (start us, length us, event | category | flops | bytes accessed | tf_op | source)
XLA Modules:
  0.0 315.0 jit_solution(1085437234150319800)
XLA Ops:
  7.2 0.0 all-gather.3.cloned.1.call-start
  7.2 1.1 pad_maximum_fusion
  8.3 15.0 %all_to_all.21 = bf16[8,16,2048]{2,1,0:T(8,128)(2,1)} all-to-all(bf16[8,16,2048]{2,1,0:T(8,128)(2,1)S(1)} %bitcast.49), channel_id=1, replica_groups=mesh['z'=4,'ylo'=2,'x'=4,'core'=2,'yhi'=2] {'x','core'}, dimensions={0} | all-to-all | bytes 1048576 | tf_op jit(solution)/shard_map/all_to_all | solution.py:33
  23.3 0.0 all-gather.3.cloned.1.call-update
  23.3 0.7 reshape.99
  24.1 1.3 fusion.19
  25.4 4.3 %all-to-all-start = ((s32[8,1,16]{2,1,0:T(1,128)}), s32[8,1,16]{2,1,0:T(1,128)S(1)}, u32[]{:S(2)}, u32[]{:S(2)}) async-start(s32[8,1,16]{2,1,0:T(1,128)} %bitcast.1), calls=%async_computation | async-start | bytes 8192 | tf_op jit(solution)/shard_map/all_to_all | solution.py:34
  29.6 0.8 select_reduce_fusion.1
  30.4 3.7 %all-to-all-done = s32[8,1,16]{2,1,0:T(1,128)S(1)} async-done(((s32[8,1,16]{2,1,0:T(1,128)}), s32[8,1,16]{2,1,0:T(1,128)S(1)}, u32[]{:S(2)}, u32[]{:S(2)}) %all-to-all-start) | async-done | bytes 544 | tf_op jit(solution)/shard_map/all_to_all | solution.py:34
  34.2 0.5 broadcast.42
  34.7 0.7 reduce.4
  35.4 0.1 reshape.109
  35.4 40.3 %all-gather = s32[16,1,128]{2,1,0:T(1,128)S(1)} all-gather(s32[1,1,128]{2,1,0:T(1,128)S(1)} %reshape.109), channel_id=1, replica_groups=mesh['z'=4,'ylo'=2,'x'=4,'core'=2,'yhi'=2] {'z','ylo','yhi'}, dimensions={0}, use_global_device_ids=true | all-gather | bytes 8704 | tf_op jit(solution)/shard_map/all_gather | solution.py:36
  75.7 0.1 select_reduce_fusion
  75.8 132.1 %all-gather.3.cloned.1.call-done = bf16[16,128,2048]{2,1,0:T(8,128)(2,1)} async-done(((bf16[1,128,2048]{2,1,0:T(8,128)(2,1)}), bf16[16,128,2048]{2,1,0:T(8,128)(2,1)}) %all-gather.3.cloned.1.call-update) | async-done | bytes 8388624 | tf_op jit(solution)/shard_map/all_gather | solution.py:35
  207.9 0.0 slice-start
  208.0 6.5 %slice_convert_fusion = (f32[16,128,1024]{2,1,0:T(8,128)}, bf16[16,128,1024]{2,1,0:T(8,128)(2,1)S(1)}) fusion(bf16[16,128,2048]{2,1,0:T(8,128)(2,1)} %all-gather.3.cloned.1.call-done), kind=kLoop, calls=%fused_computation.8 | loop fusion | flops 2097152 | bytes 20971520 | tf_op jit(solution)/shard_map/convert_element_type | solution.py:49
  214.4 0.0 copy-start
  214.4 0.0 slice-start.1
  214.4 19.2 %add_divide_fusion = (f32[2048,2048]{1,0:T(8,128)}, f32[2048,2048]{1,0:T(8,128)}) fusion(bf16[2048,1024]{1,0:T(8,128)(2,1)S(1)} %bitcast.45, bf16[1,1024,2048]{2,1,0:T(8,128)(2,1)} %param.12), kind=kOutput, calls=%fused_computation.1 | convolution fusion | flops 8602517504 | bytes 41943040 | tf_op jit(solution)/shard_map/dot_general | solution.py:46
  233.7 0.0 copy-done
  233.7 0.0 slice-done
  233.7 0.0 slice-done.1
  233.7 0.9 multiply_convert_fusion.1
  234.6 0.0 copy-start.1
  234.6 17.3 %multiply_convert_fusion = bf16[2048,2048]{1,0:T(8,128)(2,1)} fusion(f32[2048,2048]{1,0:T(8,128)} %get-tuple-element.6, bf16[2048,1024]{1,0:T(8,128)(2,1)S(1)} %bitcast.47, bf16[1,2048,1024]{2,1,0:T(8,128)(2,1)} %param.13), kind=kOutput, calls=%fused_computation | convolution fusion | flops 8627683328 | bytes 33554432 | tf_op jit(solution)/shard_map/dot_general | solution.py:50
  251.8 0.0 copy-done.1
  251.9 8.0 %fusion.14 = bf16[8,128,1024]{2,1,0:T(8,128)(2,1)} fusion(bf16[1,1024,2048]{2,1,0:T(8,128)(2,1)S(1)} %copy-done.1, bf16[8,2,128,2048]{3,2,1,0:T(8,128)(2,1)} %bitcast.53, s32[]{:T(128)S(6)} %select_n.32), kind=kOutput, calls=%fused_computation.19 | convolution fusion | flops 4296015872 | bytes 10485764 | tf_op jit(solution)/shard_map/dot_general | solution.py:58
  259.8 3.8 %all-to-all-start.2 = ((bf16[8,128,1024]{2,1,0:T(8,128)(2,1)}), bf16[8,128,1024]{2,1,0:T(8,128)(2,1)S(1)}, u32[]{:S(2)}, u32[]{:S(2)}) async-start(bf16[8,128,1024]{2,1,0:T(8,128)(2,1)} %fusion.14), calls=%async_computation.2 | async-start | bytes 4194304 | tf_op jit(solution)/shard_map/all_to_all | solution.py:62
  263.6 3.9 %fusion.1 = bf16[2048,1024]{1,0:T(8,128)(2,1)S(1)} fusion(f32[16,128,1024]{2,1,0:T(8,128)} %get-tuple-element.3, f32[2048]{0:T(1024)S(1)} %select_reduce_fusion), kind=kLoop, calls=%fused_computation.5 | loop fusion | flops 4194304 | bytes 12591104 | tf_op jit(solution)/shard_map/convert_element_type | solution.py:49
  267.5 11.5 %multiply_bitcast_fusion = f32[1,1024,1024]{2,1,0:T(8,128)} fusion(bf16[2048,1024]{1,0:T(8,128)(2,1)S(1)} %fusion.1, f32[2048,2048]{1,0:T(8,128)} %get-tuple-element.5, s32[]{:T(128)S(6)} %select_n.34, f32[2048,2048]{1,0:T(8,128)} %get-tuple-element.6), kind=kOutput, calls=%fused_computation.15 | convolution fusion | flops 4300210176 | bytes 25165828 | tf_op jit(solution)/shard_map/dot_general | solution.py:54
  279.1 10.6 %all-to-all-done.2 = bf16[8,128,1024]{2,1,0:T(8,128)(2,1)S(1)} async-done(((bf16[8,128,1024]{2,1,0:T(8,128)(2,1)}), bf16[8,128,1024]{2,1,0:T(8,128)(2,1)S(1)}, u32[]{:S(2)}, u32[]{:S(2)}) %all-to-all-start.2) | async-done | bytes 2097184 | tf_op jit(solution)/shard_map/all_to_all | solution.py:62
  289.7 1.1 reduce_sum.32
  290.8 5.9 %all-to-all-start.3 = ((bf16[8,16,1024]{2,1,0:T(8,128)(2,1)}), bf16[8,16,1024]{2,1,0:T(8,128)(2,1)S(1)}, u32[]{:S(2)}, u32[]{:S(2)}) async-start(bf16[8,16,1024]{2,1,0:T(8,128)(2,1)} %bitcast.13), calls=%async_computation.3 | async-start | bytes 524288 | tf_op jit(solution)/shard_map/all_to_all | solution.py:64
  296.7 10.6 %multiply_bitcast_fusion.1 = f32[1,512,2048]{2,1,0:T(8,128)} fusion(bf16[2048,2048]{1,0:T(8,128)(2,1)} %multiply_convert_fusion, bf16[2048,1024]{1,0:T(8,128)(2,1)} %bitcast.46, s32[]{:T(128)S(6)} %select_n.33), kind=kOutput, calls=%fused_computation.16 | convolution fusion | flops 4296015872 | bytes 14680068 | tf_op jit(solution)/shard_map/dot_general | solution.py:55
  307.3 0.0 all-to-all-done.3
  307.3 0.9 bitcast_convert_fusion
  (2 shorter events, 0.0 us)
Async XLA Ops:
  7.2 200.8 %all-gather.3.cloned.1.call-start = ((), (), s32[]{:S(2)}) async-start(), calls=%async_computation.4 | async-start | bytes 8912896 | tf_op jit(solution)/shard_map/all_gather | solution.py:35
  25.4 8.8 %all-to-all-start = ((s32[8,1,16]{2,1,0:T(1,128)}), s32[8,1,16]{2,1,0:T(1,128)S(1)}, u32[]{:S(2)}, u32[]{:S(2)}) async-start(s32[8,1,16]{2,1,0:T(1,128)} %bitcast.1), calls=%async_computation | async-start | bytes 8192 | tf_op jit(solution)/shard_map/all_to_all | solution.py:34
  207.9 25.7 %slice-start = ((s8[8388608]{0:T(1024)(128)(4,1)}), s8[4194304]{0:T(1024)(128)(4,1)S(1)}, s32[]{:S(2)}) async-start(s8[8388608]{0:T(1024)(128)(4,1)} %bitcast.43), calls=%async_computation.5 | async-start | bytes 8388608
  214.4 19.2 %copy-start = (bf16[16,128,1024]{2,1,0:T(8,128)(2,1)}, bf16[16,128,1024]{2,1,0:T(8,128)(2,1)S(1)}, u32[]{:S(2)}) copy-start(bf16[16,128,1024]{2,1,0:T(8,128)(2,1)S(1)} %get-tuple-element.4) | copy-start | bytes 12582916
  214.4 19.2 %slice-start.1 = ((s8[8388608]{0:T(1024)(128)(4,1)}), s8[4194304]{0:T(1024)(128)(4,1)S(1)}, s32[]{:S(2)}) async-start(s8[8388608]{0:T(1024)(128)(4,1)} %bitcast.43), calls=%async_computation.6 | async-start | bytes 8388608
  234.6 17.3 %copy-start.1 = (bf16[1,1024,2048]{2,1,0:T(8,128)(2,1)S(1)}, bf16[1,1024,2048]{2,1,0:T(8,128)(2,1)}, u32[]{:S(2)}) copy-start(bf16[1,1024,2048]{2,1,0:T(8,128)(2,1)} %param.12) | copy-start | bytes 12582916
  259.8 29.8 %all-to-all-start.2 = ((bf16[8,128,1024]{2,1,0:T(8,128)(2,1)}), bf16[8,128,1024]{2,1,0:T(8,128)(2,1)S(1)}, u32[]{:S(2)}, u32[]{:S(2)}) async-start(bf16[8,128,1024]{2,1,0:T(8,128)(2,1)} %fusion.14), calls=%async_computation.2 | async-start | bytes 4194304 | tf_op jit(solution)/shard_map/all_to_all | solution.py:62
  290.8 16.5 %all-to-all-start.3 = ((bf16[8,16,1024]{2,1,0:T(8,128)(2,1)}), bf16[8,16,1024]{2,1,0:T(8,128)(2,1)S(1)}, u32[]{:S(2)}, u32[]{:S(2)}) async-start(bf16[8,16,1024]{2,1,0:T(8,128)(2,1)} %bitcast.13), calls=%async_computation.3 | async-start | bytes 524288 | tf_op jit(solution)/shard_map/all_to_all | solution.py:64
Sparse Core Ops, SparseCore 0:
  23.4 184.4 all-gather.2

commit v2 on v1

v2 whole, which is shorter than its diff:
```python
import jax
import jax.numpy as jnp
from jax import lax
from jax.experimental import pallas as pl
from jax.experimental.pallas import tpu as pltpu
from jax.sharding import PartitionSpec as P

MESH = pl.DeviceIdType.MESH
F32, BF16 = jnp.float32, jnp.bfloat16
grad_scale = 0.0625

RING = 4
LINE = 8
CAP = 16
HALF = LINE * CAP // 2
PART = HALF // 2
CHUNK = 4
ROWS = CHUNK * HALF
PAIR = 2 * ROWS
NT = 512

A, B = 0, 1
ORDER = (
    (A, 0, 0), (B, 0, 0), (B, 0, 1), (B, 0, 3),
    (A, 0, 1), (A, 0, 3), (A, 1, 0), (B, 3, 0),
    (A, 1, 1), (A, 1, 3), (B, 3, 1), (B, 0, 2),
    (A, 3, 0), (A, 2, 0), (B, 1, 0), (B, 1, 1),
    (A, 0, 2), (A, 1, 2), (B, 3, 3), (B, 3, 2),
    (A, 3, 1), (A, 3, 3), (B, 1, 3), (B, 1, 2),
    (A, 2, 1), (A, 2, 3), (B, 2, 0), (B, 2, 1),
    (A, 3, 2), (A, 2, 2), (B, 2, 3), (B, 2, 2),
)
SLOT = {key: n for n, key in enumerate(ORDER)}
RS_CHUNK = {0: 0, 1: 1, 2: 2, 4: 3}
RS_SLOT = {key: RS_CHUNK[n // CHUNK] * CHUNK + n % CHUNK for key, n in SLOT.items() if n // CHUNK in RS_CHUNK}


def hops():
    table = {}

    def add(name, axis, half, dy, dz, split):
        for sign in (1, -1):
            if split:
                if axis == "y":
                    dy_s, dz_s = (-sign * dy) % RING, dz
                else:
                    dy_s, dz_s = dy, (-sign * dz) % RING
                part = 0 if sign == 1 else 1
            else:
                dy_s, dz_s, part = dy, dz, None
            there = (half, (dy_s - sign) % RING, dz_s) if axis == "y" else (half, dy_s, (dz_s - sign) % RING)
            table.setdefault(name, []).append((axis, sign, (half, dy_s, dz_s), part, there))

    add("y1", "y", A, 0, 0, False)
    add("y2", "y", B, 0, 0, False)
    add("y3", "y", A, 1, 0, True)
    add("y4", "y", B, 0, 1, False)
    add("y5", "y", B, 0, 3, False)
    add("y6", "y", B, 0, 2, False)
    add("y7", "y", B, 1, 0, True)
    add("y8", "y", B, 1, 1, True)
    add("y9", "y", B, 1, 3, True)
    add("y10", "y", B, 1, 2, True)
    add("z1", "z", B, 0, 0, False)
    add("z2", "z", A, 0, 0, False)
    add("z3", "z", B, 0, 1, True)
    add("z4", "z", A, 1, 0, False)
    add("z7", "z", A, 3, 0, False)
    add("z5", "z", A, 0, 1, True)
    add("z6", "z", A, 1, 1, True)
    add("z8", "z", A, 2, 0, False)
    add("z9", "z", A, 3, 1, True)
    add("z10", "z", A, 2, 1, True)
    return table


HOPS = hops()
HOP_SEM = {name: 2 * n for n, name in enumerate(HOPS)}


def kernel(
    x_hbm, cot_hbm, tag_hbm, gate_smem, w1_hbm, w2_hbm,
    home_hbm, gin_hbm, gout_hbm,
    rows, w1, w2, w1t, w2t, sc, act, pg, xt, actt, gin, gout, gates, tag_line, tag_all,
    rgb, ys, ry, zs, zq, zr, fs, home, home32,
    local_sem, tagp_sem, tagp_send, line_sem, line_send, tag_sem, tag_send, slot_sem, hop_send,
    ry_sem, ry_send, zq_sem, zq_send, zr_sem, zr_send, home_sem, home_send, out_sem,
):
    blk, yhi = lax.axis_index("blk"), lax.axis_index("dp")
    c = blk % 2
    x = (blk // 2) % RING
    y = yhi * 2 + (blk // LINE) % 2
    z = blk // (2 * LINE)
    me = x * 2 + c

    def on_line(j):
        return ((z * 2 + y % 2) * LINE + j, yhi)

    def on_plane(dy, dz):
        ty, tz = (y + dy) % RING, (z + dz) % RING
        return ((tz * 2 + ty % 2) * LINE + me, ty // 2)

    def weight_copy(n):
        return pltpu.make_async_copy((w1_hbm, w2_hbm)[n], (w1, w2)[n], local_sem.at[n])

    def line_copies(step):
        j = (me + step) % LINE
        here = pl.ds(pl.multiple_of(j * CAP, CAP), CAP)
        slot = me // CHUNK
        there = pl.ds(pl.multiple_of((me % CHUNK) * CAP, CAP), CAP)
        out = []
        for kind, src in ((0, x_hbm), (1, cot_hbm)):
            out.append((src.at[here], rows.at[slot, kind, there], line_sem.at[me, kind], line_send.at[step, kind], j))
        return (tag_hbm.at[j], tag_line.at[me], tagp_sem.at[me], tagp_send.at[step], j), out

    def remote(src, dst, recv, send, device):
        return pltpu.make_async_remote_copy(
            src_ref=src, dst_ref=dst, send_sem=send, recv_sem=recv, device_id=device, device_id_type=MESH
        )

    def line_remote(spec):
        src, dst, recv, send, j = spec
        return remote(src, dst, recv, send, on_line(j))

    def hop_copy(name, n):
        axis, sign, here, part, there = HOPS[name][n]
        src, dst = rows.at[SLOT[here]], rows.at[SLOT[there]]
        if part is not None:
            span = pl.ds(part * PART, PART)
            src, dst = rows.at[SLOT[here], :, span], rows.at[SLOT[there], :, span]
        device = on_plane(sign, 0) if axis == "y" else on_plane(0, sign)
        return remote(src, dst, slot_sem.at[SLOT[there]], hop_send.at[HOP_SEM[name] + n], device)

    def send_hops(*names):
        for name in names:
            for n in range(2):
                hop_copy(name, n).start()

    def wait_slots(*keys):
        for key in keys:
            n = SLOT[key]
            pltpu.make_async_copy(rows.at[n], rows.at[n], slot_sem.at[n]).wait()

    def y_copy(half, dz):
        return remote(
            ys.at[half, dz], ry.at[half, dz], ry_sem.at[half, dz], ry_send.at[half, dz], on_plane(1 if half == A else 3, 0)
        )

    def y_send(*keys):
        for half, dz in keys:
            ys[half, dz] = rgb[RS_SLOT[(half, 1 if half == A else 3, dz)]].astype(BF16)
        for half, dz in keys:
            y_copy(half, dz).start()

    def relay_copy(half):
        return remote(zs.at[half, 0], zq.at[half], zq_sem.at[half], zq_send.at[half], on_plane(0, 1 if half == A else 3))

    def z_copy(half, dz):
        n = 0 if dz == 1 else 1
        return remote(zs.at[half, 1 + n], zr.at[half, n], zr_sem.at[half, n], zr_send.at[half, n], on_plane(0, dz))

    def total(half, dz):
        pltpu.make_async_copy(ry.at[half, dz], ry.at[half, dz], ry_sem.at[half, dz]).wait()
        return rgb[RS_SLOT[(half, 0, dz)]] + ry[half, dz].astype(F32)

    def transpose_weights():
        def body(i, _):
            cols = pl.ds(pl.multiple_of(i * 256, 256), 256)
            w2t[:, cols] = w2[cols, :].T
            w1t[cols, :] = w1[:, cols].T
            return 0

        lax.fori_loop(0, w1.shape[1] // 256, body, 0)

    def make_gates():
        row = lax.broadcasted_iota(jnp.int32, (HALF, 128), 0)
        lane = lax.broadcasted_iota(jnp.int32, (HALF, 128), 1)
        for n, (half, dy, dz) in enumerate(ORDER):
            tags = tag_all[dy * RING + dz][0:1, :]
            lanes = jnp.zeros_like(tags)
            for task in range(4):
                lanes = jnp.where(tags == float(task), gate_smem[0, task], lanes)
            picked = jnp.where(lane == row + half * HALF, jnp.broadcast_to(lanes, (HALF, 128)), 0.0)
            gates[n] = jnp.broadcast_to(jnp.sum(picked, axis=1, keepdims=True), (HALF, 128))

    def forward(k):
        four = pl.ds(k * CHUNK, CHUNK)
        span = pl.ds(pl.multiple_of((k % 2) * ROWS, ROWS), ROWS)
        gate = gates[four].reshape(ROWS, 128)
        for n in range(rows.shape[3] // 128):
            cols = pl.ds(n * 128, 128)
            cot = rows[four, 1, :, cols].reshape(ROWS, 128).astype(F32)
            sc[span, cols] = (gate * cot).astype(BF16)

        def body(n, _):
            cols = pl.ds(pl.multiple_of(n * NT, NT), NT)
            pre = jnp.dot(rows[four, 0].reshape(ROWS, rows.shape[3]), w1[:, cols], preferred_element_type=F32)
            back = jnp.dot(sc[span, :], w2t[:, cols], preferred_element_type=F32)
            sig = 0.5 * jnp.tanh(0.5 * pre) + 0.5
            value = pre * sig
            act[span, cols] = value.astype(BF16)
            pg[span, cols] = (back * (sig + value * (1.0 - sig))).astype(BF16)
            return 0

        lax.fori_loop(0, w1.shape[1] // NT, body, 0)

    def row_grads(k, r):
        span = pl.ds(pl.multiple_of((k % 2) * ROWS, ROWS), ROWS)

        def body(n, _):
            cols = pl.ds(pl.multiple_of(n * NT, NT), NT)
            part = jnp.dot(pg[span, :], w1t[:, cols], preferred_element_type=F32)
            rgb[pl.ds(r * CHUNK, CHUNK), :, cols] = part.reshape(CHUNK, HALF, NT)
            return 0

        lax.fori_loop(0, w1t.shape[1] // NT, body, 0)

    def turn(k):
        eight = pl.ds((k - 1) * CHUNK, 2 * CHUNK)
        width = xt.shape[0]
        for n in range(width // 256):
            cols = pl.ds(pl.multiple_of(yhi * width + n * 256, 256), 256)
            xt[pl.ds(n * 256, 256), :] = rows[eight, 0, :, cols].reshape(PAIR, 256).T
        width = actt.shape[0]
        for n in range(width // 256):
            cols = pl.ds(pl.multiple_of(yhi * width + n * 256, 256), 256)
            actt[pl.ds(n * 256, 256), :] = act[:, cols].T

    def grads():
        def body_in(n, _):
            cols = pl.ds(pl.multiple_of(n * NT, NT), NT)
            gin[:, cols] += jnp.dot(xt[...], pg[:, cols], preferred_element_type=F32)
            return 0

        def body_out(n, _):
            cols = pl.ds(pl.multiple_of(n * 256, 256), 256)
            gout[:, cols] += jnp.dot(actt[...], sc[:, cols], preferred_element_type=F32)
            return 0

        lax.fori_loop(0, gin.shape[1] // NT, body_in, 0)
        lax.fori_loop(0, gout.shape[1] // 256, body_out, 0)

    def out_copy(which, n):
        acc, hbm = ((gin, gin_hbm), (gout, gout_hbm))[which]
        span = pl.ds(pl.multiple_of(n * 128, 128), 128)
        return pltpu.make_async_copy(acc.at[span], hbm.at[span], out_sem.at[which])

    def last_grads():
        def body_in(n, _):
            span = pl.ds(pl.multiple_of(n * 128, 128), 128)
            gin[span, :] = (gin[span, :] + jnp.dot(xt[span, :], pg[...], preferred_element_type=F32)) * grad_scale
            out_copy(0, n).start()
            return 0

        def body_out(n, _):
            span = pl.ds(pl.multiple_of(n * 128, 128), 128)
            gout[span, :] = (gout[span, :] + jnp.dot(actt[span, :], sc[...], preferred_element_type=F32)) * grad_scale
            out_copy(1, n).start()
            return 0

        lax.fori_loop(0, gin.shape[0] // 128, body_in, 0)
        lax.fori_loop(0, gout.shape[0] // 128, body_out, 0)

    for n in range(2):
        weight_copy(n).start()
    tag_own, own = line_copies(0)
    pltpu.make_async_copy(tag_own[0], tag_own[1], tag_own[2]).start()
    for spec in own:
        pltpu.make_async_copy(spec[0], spec[1], spec[2]).start()

    barrier = pltpu.get_barrier_semaphore()
    for step in range(1, LINE):
        pl.semaphore_signal(barrier, inc=1, device_id=on_line((me + step) % LINE), device_id_type=MESH)
    for dy in range(RING):
        for dz in range(RING):
            if dy or dz:
                pl.semaphore_signal(barrier, inc=1, device_id=on_plane(dy, dz), device_id_type=MESH)
    pl.semaphore_wait(barrier, LINE - 1 + RING * RING - 1)

    for step in range(1, LINE):
        line_remote(line_copies(step)[0]).start()
    for step in range(1, LINE):
        for spec in line_copies(step)[1]:
            line_remote(spec).start()

    gin[...] = jnp.zeros_like(gin)
    gout[...] = jnp.zeros_like(gout)

    for j in range(LINE):
        pltpu.make_async_copy(tag_line.at[j], tag_line.at[j], tagp_sem.at[j]).wait()
    tags = tag_line[0]
    for j in range(1, LINE):
        tags = tags + tag_line[j]
    tag_all[0] = tags

    def tag_copy(dy, dz):
        there = ((-dy) % RING) * RING + (-dz) % RING
        return remote(tag_all.at[0], tag_all.at[there], tag_sem, tag_send, on_plane(dy, dz))

    around = [(dy, dz) for dy in range(RING) for dz in range(RING) if dy or dz]
    for dy, dz in around:
        tag_copy(dy, dz).start()

    def wait_line(half):
        for j in range(half * CHUNK, half * CHUNK + CHUNK):
            for kind in range(2):
                part = rows.at[half, kind, pl.ds((j % CHUNK) * CAP, CAP)]
                pltpu.make_async_copy(part, part, line_sem.at[j, kind]).wait()

    wait_line(A)
    wait_line(B)
    send_hops("y1", "z1", "y2", "z2")

    for n in range(2):
        weight_copy(n).wait()
    transpose_weights()
    others = tag_all.at[pl.ds(1, RING * RING - 1)]
    pltpu.make_async_copy(others, others, tag_sem).wait()
    make_gates()

    def step(k, _):
        @pl.when(k == 0)
        def _():
            wait_slots((A, 1, 0), (A, 3, 0), (B, 0, 1), (B, 0, 3))
            send_hops("y3", "z3", "y4", "z4", "y5", "z7")

        @pl.when(k == 1)
        def _():
            wait_slots((B, 1, 0), (B, 3, 0), (A, 0, 1), (A, 0, 3))
            send_hops("z5")

        @pl.when(k == 2)
        def _():
            wait_slots((B, 1, 1), (B, 3, 1), (A, 1, 1), (A, 1, 3))
            send_hops("z6", "y8", "z8")

        @pl.when(k == 4)
        def _():
            wait_slots((B, 1, 2), (B, 3, 2), (A, 0, 2), (A, 1, 2))
            send_hops("y10")

        @pl.when(k == 6)
        def _():
            wait_slots((B, 2, 0), (B, 2, 1))

        @pl.when(k == 7)
        def _():
            wait_slots((A, 3, 2), (A, 2, 2), (B, 2, 3), (B, 2, 2))

        forward(k)

        @pl.when(k == 1)
        def _():
            wait_slots((A, 2, 0), (B, 0, 2))
            send_hops("y6", "y7")

        @pl.when(k == 3)
        def _():
            wait_slots((A, 3, 1), (A, 3, 3), (B, 1, 3), (B, 3, 3))
            send_hops("z9", "y9")

        @pl.when(k == 5)
        def _():
            wait_slots((A, 2, 1), (A, 2, 3))
            send_hops("z10")

        @pl.when(k == 6)
        def _():
            for half, dz in ((A, 1), (B, 3)):
                pltpu.make_async_copy(zq.at[half], zq.at[half], zq_sem.at[half]).wait()
                zs[half, 1 if dz == 1 else 2] = (total(half, dz) + zq[half].astype(F32)).astype(BF16)
            z_copy(A, 1).start()
            z_copy(B, 3).start()

        @pl.when(k == 7)
        def _():
            for half in (A, B):
                value = total(half, 0)
                for n in range(2):
                    pltpu.make_async_copy(zr.at[half, n], zr.at[half, n], zr_sem.at[half, n]).wait()
                    value = value + zr[half, n].astype(F32)
                fs[pl.ds(half * HALF, HALF), :] = value.astype(BF16)
            for n in range(LINE):
                home_copy(n).start() if n else home_local().start()

        @pl.when((k < 3) | (k == 4))
        def _():
            row_grads(k, k - k // 4)

        @pl.when(k == 1)
        def _():
            y_send((A, 0), (B, 0))

        @pl.when(k == 2)
        def _():
            y_send((A, 1), (A, 3), (B, 1))

        @pl.when(k == 4)
        def _():
            y_send((A, 2), (B, 2), (B, 3))

        @pl.when(k % 2 == 1)
        def _():
            turn(k)

            @pl.when(k < 7)
            def _():
                grads()

            @pl.when(k == 7)
            def _():
                last_grads()

        @pl.when(k == 3)
        def _():
            for half, dz in ((A, 3), (B, 1)):
                zs[half, 1 if dz == 1 else 2] = total(half, dz).astype(BF16)
            z_copy(A, 3).start()
            z_copy(B, 1).start()

        @pl.when(k == 5)
        def _():
            for half in (A, B):
                zs[half, 0] = total(half, 2).astype(BF16)
            for half in (A, B):
                relay_copy(half).start()

        return 0

    def home_copy(step):
        j = (me + step) % LINE
        return remote(
            fs.at[pl.ds(pl.multiple_of(j * CAP, CAP), CAP)],
            home.at[pl.ds(pl.multiple_of(me * CAP, CAP), CAP)],
            home_sem.at[me],
            home_send.at[step],
            on_line(j),
        )

    def home_local():
        span = pl.ds(pl.multiple_of(me * CAP, CAP), CAP)
        home[span, :] = fs[span, :]
        return home_nothing

    class home_nothing:
        start = staticmethod(lambda: None)

    lax.fori_loop(0, len(ORDER) // CHUNK, step, 0)

    for n in range(1, LINE):
        span = pl.ds(pl.multiple_of(((me + n) % LINE) * CAP, CAP), CAP)
        pltpu.make_async_copy(home.at[span], home.at[span], home_sem.at[(me + n) % LINE]).wait()
    home32[...] = home[...].astype(F32)
    pltpu.make_async_copy(home32, home_hbm, local_sem.at[2]).start()

    for step_n in range(1, LINE):
        tag_spec, specs = line_copies(step_n)
        line_remote(tag_spec).wait_send()
        for spec in specs:
            line_remote(spec).wait_send()
        home_copy(step_n).wait_send()
    pltpu.make_async_copy(others, others, tag_send).wait()
    for name in HOPS:
        for n in range(2):
            hop_copy(name, n).wait_send()
    for half in (A, B):
        for dz in range(RING):
            y_copy(half, dz).wait_send()
        relay_copy(half).wait_send()
        for dz in (1, 3):
            z_copy(half, dz).wait_send()
    pltpu.make_async_copy(home32, home_hbm, local_sem.at[2]).wait()
    pltpu.make_async_copy(gin, gin_hbm, out_sem.at[0]).wait()
    pltpu.make_async_copy(gout, gout_hbm, out_sem.at[1]).wait()


def on_device(inputs, cotangent, task_ids, group_counts, task_gate, w_in, w_out):
    groups = group_counts.shape[1]
    width = inputs.shape[1]
    hidden = w_in.shape[2]
    tasks = task_gate.shape[0]
    blk = lax.axis_index("blk")
    match = jnp.arange(task_gate.shape[1], dtype=jnp.int32) == blk
    gate_column = jnp.sum(jnp.where(match[None, :], task_gate, 0.0), axis=1).reshape(1, tasks)
    live = jnp.arange(CAP, dtype=jnp.int32)[None, :] < group_counts[0][:, None]
    tags = jnp.where(live, task_ids.reshape(groups, CAP), tasks).astype(F32)
    lane = jnp.arange(LINE * CAP, dtype=jnp.int32)
    tags = jnp.where((lane // CAP == blk % LINE)[None, :], jnp.tile(tags, (1, LINE)), 0.0)
    tags = jnp.broadcast_to(tags[:, None, :], (groups, 8, LINE * CAP))
    any_space = pl.BlockSpec(memory_space=pl.ANY)
    dma = pltpu.SemaphoreType.DMA
    home, gin, gout = pl.pallas_call(
        kernel,
        out_shape=(
            jax.ShapeDtypeStruct((groups * CAP, width), F32),
            jax.ShapeDtypeStruct((width // 2, hidden), F32),
            jax.ShapeDtypeStruct((hidden // 2, width), F32),
        ),
        in_specs=[any_space] * 3 + [pl.BlockSpec(memory_space=pltpu.SMEM)] + [any_space] * 2,
        out_specs=(any_space,) * 3,
        scratch_shapes=[
            pltpu.VMEM((len(ORDER), 2, HALF, width), BF16),
            pltpu.VMEM((width, hidden), BF16),
            pltpu.VMEM((hidden, width), BF16),
            pltpu.VMEM((hidden, width), BF16),
            pltpu.VMEM((width, hidden), BF16),
            pltpu.VMEM((PAIR, width), BF16),
            pltpu.VMEM((PAIR, hidden), BF16),
            pltpu.VMEM((PAIR, hidden), BF16),
            pltpu.VMEM((width // 2, PAIR), BF16),
            pltpu.VMEM((hidden // 2, PAIR), BF16),
            pltpu.VMEM((width // 2, hidden), F32),
            pltpu.VMEM((hidden // 2, width), F32),
            pltpu.VMEM((len(ORDER), HALF, 128), F32),
            pltpu.VMEM((LINE, 8, LINE * CAP), F32),
            pltpu.VMEM((RING * RING, 8, LINE * CAP), F32),
            pltpu.VMEM((16, HALF, width), F32),
            pltpu.VMEM((2, RING, HALF, width), BF16),
            pltpu.VMEM((2, RING, HALF, width), BF16),
            pltpu.VMEM((2, 3, HALF, width), BF16),
            pltpu.VMEM((2, HALF, width), BF16),
            pltpu.VMEM((2, 2, HALF, width), BF16),
            pltpu.VMEM((2 * HALF, width), BF16),
            pltpu.VMEM((2 * HALF, width), BF16),
            pltpu.VMEM((2 * HALF, width), F32),
            dma((3,)),
            dma((LINE,)),
            dma((LINE,)),
            dma((LINE, 2)),
            dma((LINE, 2)),
            dma(()),
            dma(()),
            dma((len(ORDER),)),
            dma((2 * len(HOPS),)),
            dma((2, RING)),
            dma((2, RING)),
            dma((2,)),
            dma((2,)),
            dma((2, 2)),
            dma((2, 2)),
            dma((LINE,)),
            dma((LINE,)),
            dma((2,)),
        ],
        compiler_params=pltpu.CompilerParams(
            collective_id=0, has_side_effects=True, vmem_limit_bytes=63 * 1024 * 1024
        ),
    )(inputs, cotangent, tags, gate_column, w_in[0], w_out[0])
    return home, gin[None], gout[None]


def solution(mesh):
    in_specs = (
        P(("blk", "dp"), None),
        P(("blk", "dp"), None),
        P(("blk", "dp")),
        P(("blk", "dp"), None),
        P(),
        P("blk", None, None),
        P("blk", None, None),
    )
    out_specs = (P(("blk", "dp"), None), P("blk", "dp", None), P("blk", "dp", None))
    return jax.shard_map(on_device, mesh=mesh, in_specs=in_specs, out_specs=out_specs, check_vma=False)
```

time: 316 us -> 108 us (0.34)
  waiting for transfers between devices: 146 us -> 0 us
  Pallas kernels: 0 us -> 95 us
  matrix products: 66.6 us -> 0 us
  blocking collectives: 55.3 us -> 0 us
  other arithmetic: 17.1 us -> 2.06 us
  starting transfers between devices: 14 us -> 0 us
  between operations: 14.1 us -> 0.67 us
  local copies, waits for them, and re-layouts: 1.34 us -> 10.2 us
    all_gather x1 -> x0, waiting for transfers between devices: 132 us -> none  [on_device(): lax.all_gather(both.reshape(groups * cap, 2 * width), PLANE, axis=0, tile...]
    pallas_call x0 -> x1, Pallas kernels: none -> 95 us  [on_device(): pl.pallas_call(kernel, out_shape=(jax.ShapeDtypeStruct((groups * CAP, wid...]
    dot_general x5 -> x0, matrix products: 66.6 us -> none  [the longest x1 19.2 us: on_device(): pre = jnp.dot(x, w1, preferred_element_type=jnp.float32)]
    all_gather x1 -> x0, blocking collectives: 40.3 us -> none  [on_device(): lax.all_gather(tags.reshape(groups * cap), PLANE, axis=0, tiled=False)]
    all_to_all x1 -> x0, blocking collectives: 15 us -> none  [on_device(): both = lax.all_to_all(both, LINE, split_axis=0, concat_axis=0, tiled=True)]
    all_to_all x3 -> x0, waiting for transfers between devices: 14.3 us -> none  [the longest x1 10.6 us: on_device(): lax.all_to_all(row_grad, ('z', 'ylo'), split_axis=0, concat_axis=0, tiled...]
    all_to_all x3 -> x0, starting transfers between devices: 13.9 us -> none  [the longest x1 5.91 us: on_device(): lax.all_to_all(row_grad.reshape(groups, cap, width), LINE, split_axis=0,...]
    convert_element_type x3 -> x1, other arithmetic: 11.2 us -> 0.73 us  [on_device(): tags = jnp.where(live, task_ids.reshape(groups, CAP), tasks).astype(F32)]
  transfers between devices with their start and end apart: 4 -> 0, of which waited for: 3 -> 0; matrix products, arithmetic and copies ran while one was open for 10% -> 0% of each run, Pallas kernels for 0% -> 0%
where the time goes in v2:
time: 108 us
  Pallas kernels  95 us (88%)
  local copies, waits for them, and re-layouts  10.2 us (9%)
  other arithmetic  2.06 us (2%)
    pallas_call x1, Pallas kernels, on_device(): pl.pallas_call(kernel, out_shape=(jax.ShapeDtypeStruct((groups * CAP, wid...  95 us
    unnamed x5, local copies, waits for them, and re-layouts  8.75 us

profile of v2, /device:TPU:1, one launch (start us, length us, event | category | flops | bytes accessed | tf_op | source)
XLA Modules:
  0.0 108.0 jit_solution(16713423450926059294)
XLA Ops:
  0.7 1.3 %select_reduce_fusion = f32[4]{0:T(128)} fusion(f32[4,64]{1,0:T(4,128)} %param.11, pred[64]{0:T(512)(128)(4,1)S(1)} %iota_compare_fusion.1), kind=kLoop, calls=%fused_computation.2 | loop fusion | flops 508 | bytes 1104 | tf_op jit(solution)/shard_map/reduce_sum | solution.py:484
  2.0 0.7 reshape.77
  2.7 0.7 select_convert_fusion
  3.4 0.1 tile.10
  3.5 0.6 broadcast_in_dim.46.tag_hbm
  4.2 95.0 %shard_map.94 = (f32[128,1024]{1,0:T(8,128)}, f32[512,2048]{1,0:T(8,128)}, f32[1024,1024]{1,0:T(8,128)}) custom-call(bf16[128,1024]{1,0:T(8,128)(2,1)} %x_hbm.1, bf16[128,1024]{1,0:T(8,128)(2,1)} %cot_hbm.1, f32[8,8,128]{2,1,0:T(8,128)} %broadcast_in_dim.46.tag_hbm, f32[1,4]{1,0:T(1,128)} %bitcast.10, bf16[1024,2048]{1,0:T(8,128)(2,1)} %bitcast.6, ...), custom_call_target="tpu_custom_call" | custom-call | tf_op jit(solution)/shard_map/pallas_call | solution.py:492
  99.2 1.9 %copy.13 = f32[128,1024]{1,0:T(8,128)} copy(f32[128,1024]{1,0:T(8,128)} %get-tuple-element.12) | data formatting | bytes 1048576
  101.1 0.0 copy-start
  101.1 4.8 %copy.14 = f32[1,512,2048]{2,1,0:T(8,128)} copy(f32[1,512,2048]{2,1,0:T(8,128)} %bitcast.9) | data formatting | bytes 8388608
  105.9 0.0 copy-done
  105.9 2.0 %copy.15 = f32[1,1024,1024]{2,1,0:T(8,128)} copy(f32[1,1024,1024]{2,1,0:T(8,128)S(1)} %bitcast.8) | data formatting | bytes 8388608
  (4 shorter events, 0.0 us)
Async XLA Ops:
  101.1 4.9 %copy-start = (f32[1024,1024]{1,0:T(8,128)S(1)}, f32[1024,1024]{1,0:T(8,128)}, u32[]{:S(2)}) copy-start(f32[1024,1024]{1,0:T(8,128)} %get-tuple-element.8) | copy-start | bytes 12582916

commit v3 on v2

v3 whole, which is shorter than its diff:
```python
import jax
import jax.numpy as jnp
from jax import lax
from jax.experimental import pallas as pl
from jax.experimental.pallas import tpu as pltpu
from jax.sharding import PartitionSpec as P

MESH = pl.DeviceIdType.MESH
F32, BF16 = jnp.float32, jnp.bfloat16
grad_scale = 0.0625

RING = 4
LINE = 8
CAP = 16
HALF = LINE * CAP // 2
PART = HALF // 2
CHUNK = 4
ROWS = CHUNK * HALF
PAIR = 2 * ROWS
NT = 512
VMEM_LIMIT = 46 * 1024 * 1024

A, B = 0, 1
ORDER = (
    (A, 0, 0), (B, 0, 0), (A, 0, 1), (A, 0, 3),
    (A, 1, 0), (B, 0, 1), (B, 0, 3), (B, 3, 0),
    (A, 1, 1), (A, 1, 3), (B, 3, 1), (B, 0, 2),
    (A, 0, 2), (A, 1, 2), (B, 3, 3), (B, 3, 2),
    (A, 3, 0), (B, 1, 0), (B, 1, 1), (B, 1, 3),
    (A, 2, 0), (B, 1, 2), (A, 3, 1), (A, 3, 3),
    (A, 2, 1), (A, 2, 3), (B, 2, 0), (B, 2, 1),
    (A, 3, 2), (A, 2, 2), (B, 2, 3), (B, 2, 2),
)
SLOT = {key: n for n, key in enumerate(ORDER)}
OWED = 4


def place(r, q):
    return {0: 0, 1: 2, 3: 4, 2: 6}[r] + q


STEPS = ((0, 1), (1, 0), (3, 0), (1, 1), (3, 1), (2, 0), (2, 1))


def hops():
    table = {}

    def add(name, axis, half, dy, dz, split):
        for sign in (1, -1):
            if split:
                if axis == "y":
                    dy_s, dz_s = (-sign * dy) % RING, dz
                else:
                    dy_s, dz_s = dy, (-sign * dz) % RING
                part = 0 if sign == 1 else 1
            else:
                dy_s, dz_s, part = dy, dz, None
            there = (half, (dy_s - sign) % RING, dz_s) if axis == "y" else (half, dy_s, (dz_s - sign) % RING)
            table.setdefault(name, []).append((axis, sign, (half, dy_s, dz_s), part, there))

    add("y1", "y", A, 0, 0, False)
    add("y2", "y", B, 0, 0, False)
    add("y3", "y", A, 1, 0, True)
    add("y4", "y", B, 0, 1, False)
    add("y5", "y", B, 0, 3, False)
    add("y6", "y", B, 0, 2, False)
    add("y7", "y", B, 1, 0, True)
    add("y8", "y", B, 1, 1, True)
    add("y9", "y", B, 1, 3, True)
    add("y10", "y", B, 1, 2, True)
    add("z1", "z", B, 0, 0, False)
    add("z2", "z", A, 0, 0, False)
    add("z3", "z", B, 0, 1, True)
    add("z4", "z", A, 1, 0, False)
    add("z7", "z", A, 3, 0, False)
    add("z5", "z", A, 0, 1, True)
    add("z6", "z", A, 1, 1, True)
    add("z8", "z", A, 2, 0, False)
    add("z9", "z", A, 3, 1, True)
    add("z10", "z", A, 2, 1, True)
    return table


HOPS = hops()
HOP_SEM = {name: 2 * n for n, name in enumerate(HOPS)}


def kernel(
    x_hbm, cot_hbm, ids_ref, count_smem, gate_smem, w1_hbm, w2_hbm,
    home_ref, gin, gout,
    rows, w1, w2, w1t, w2t, sc, act, pg, xt, actt, gates, tag_out, tag_line, tag_all,
    rgb, ys, ry, zs, zq, zr, fs, home,
    local_sem, tagp_sem, tagp_send, line_sem, line_send, tag_sem, tag_send, slot_sem, hop_send,
    ry_sem, ry_send, zq_sem, zq_send, zr_sem, zr_send, home_sem, home_send,
):
    blk, yhi = lax.axis_index("blk"), lax.axis_index("dp")
    c = blk % 2
    x = (blk // 2) % RING
    y = yhi * 2 + (blk // LINE) % 2
    z = blk // (2 * LINE)
    me = x * 2 + c

    def line_index(dr, dq):
        return ((x + dr) % RING) * 2 + (c + dq) % 2

    def on_line(dr, dq):
        return ((z * 2 + y % 2) * LINE + line_index(dr, dq), yhi)

    def on_plane(dy, dz):
        ty, tz = (y + dy) % RING, (z + dz) % RING
        return ((tz * 2 + ty % 2) * LINE + me, ty // 2)

    def remote(src, dst, recv, send, device):
        return pltpu.make_async_remote_copy(
            src_ref=src, dst_ref=dst, send_sem=send, recv_sem=recv, device_id=device, device_id_type=MESH
        )

    def arrive(ref, sem):
        pltpu.make_async_copy(ref, ref, sem).wait()

    def weight_copy(n):
        return pltpu.make_async_copy((w1_hbm, w2_hbm)[n], (w1, w2)[n], local_sem.at[n])

    def cap_rows(j):
        return pl.ds(pl.multiple_of(j * CAP, CAP), CAP)

    def piece(n):
        return n // CHUNK, pl.ds((n % CHUNK) * CAP, CAP)

    def line_copies(dr, dq):
        there = place((-dr) % RING, dq)
        here = cap_rows(line_index(dr, dq))
        slot, span = piece(there)
        for kind, src in ((0, x_hbm), (1, cot_hbm)):
            if (dr, dq) == (0, 0):
                yield pltpu.make_async_copy(src.at[here], rows.at[slot, kind, span], line_sem.at[there])
            else:
                send = line_send.at[there, kind]
                yield remote(src.at[here], rows.at[slot, kind, span], line_sem.at[there], send, on_line(dr, dq))

    def tag_line_copy(dr, dq):
        there = place((-dr) % RING, dq)
        return remote(tag_out.at[there], tag_line.at[there], tagp_sem.at[there], tagp_send.at[there], on_line(dr, dq))

    def tag_copy(dy, dz):
        there = ((-dy) % RING) * RING + (-dz) % RING
        return remote(tag_all.at[0], tag_all.at[there], tag_sem, tag_send, on_plane(dy, dz))

    def hop_copy(name, n, span=None):
        axis, sign, here, part, there = HOPS[name][n]
        if part is not None:
            span = pl.ds(part * PART, PART)
        src, dst = rows.at[SLOT[here]], rows.at[SLOT[there]]
        if span is not None:
            src, dst = rows.at[SLOT[here], :, span], rows.at[SLOT[there], :, span]
        device = on_plane(sign, 0) if axis == "y" else on_plane(0, sign)
        return remote(src, dst, slot_sem.at[SLOT[there]], hop_send.at[HOP_SEM[name] + n], device)

    def send_hops(*names):
        for name in names:
            for n in range(2):
                hop_copy(name, n).start()

    def send_piece(n):
        half, span = piece(n)
        arrive(rows.at[half, :, span], line_sem.at[n])
        for name in (("y1", "z2"), ("y2", "z1"))[half]:
            for m in range(2):
                hop_copy(name, m, span).start()

    def wait_slots(*keys):
        for key in keys:
            arrive(rows.at[SLOT[key]], slot_sem.at[SLOT[key]])

    def y_copy(half, dz):
        device = on_plane(1 if half == A else 3, 0)
        return remote(ys.at[half, dz], ry.at[half, dz], ry_sem.at[half, dz], ry_send.at[half, dz], device)

    def y_send(*keys):
        for half, dz in keys:
            ys[half, dz] = rgb[SLOT[(half, 1 if half == A else 3, dz)]].astype(BF16)
        for half, dz in keys:
            y_copy(half, dz).start()

    def relay_copy(half):
        return remote(zs.at[half, 0], zq.at[half], zq_sem.at[half], zq_send.at[half], on_plane(0, 1 if half == A else 3))

    def z_copy(half, dz):
        n = 0 if dz == 1 else 1
        return remote(zs.at[half, 1 + n], zr.at[half, n], zr_sem.at[half, n], zr_send.at[half, n], on_plane(0, dz))

    def home_copy(dr, dq):
        n = place(dr, dq)
        there = place((-dr) % RING, dq)
        src = fs.at[pl.ds(n * CAP, CAP)]
        return remote(src, home.at[cap_rows(me)], home_sem.at[there], home_send.at[n], on_line(dr, dq))

    def total(half, dz):
        arrive(ry.at[half, dz], ry_sem.at[half, dz])
        return rgb[SLOT[(half, 0, dz)]] + ry[half, dz].astype(F32)

    def transpose_weights():
        def body(i, _):
            cols = pl.ds(pl.multiple_of(i * 256, 256), 256)
            w2t[:, cols] = w2[cols, :].T
            w1t[cols, :] = w1[:, cols].T
            return 0

        lax.fori_loop(0, w1.shape[1] // 256, body, 0)

    def make_tags():
        lane = lax.broadcasted_iota(jnp.int32, (8, 128), 1)
        count = jnp.zeros_like(lane)
        for group in range(LINE):
            count = jnp.where(lane // CAP == group, count_smem[0, group], count)
        tags = jnp.where(lane % CAP < count, jnp.broadcast_to(ids_ref[...], (8, 128)), 4).astype(F32)
        for dr, dq in ((0, 0),) + STEPS:
            n = place((-dr) % RING, dq)
            shift = ((n - line_index(dr, dq)) * CAP) % 128
            moved = jnp.where(lane // CAP == n, pltpu.roll(tags, shift, 1), 0.0)
            (tag_line if n == 0 else tag_out)[n] = moved

    def make_gates():
        row = lax.broadcasted_iota(jnp.int32, (HALF, 128), 0)
        lane = lax.broadcasted_iota(jnp.int32, (HALF, 128), 1)
        for n, (half, dy, dz) in enumerate(ORDER):
            tags = tag_all[dy * RING + dz][0:1, :]
            lanes = jnp.zeros_like(tags)
            for task in range(4):
                lanes = jnp.where(tags == float(task), gate_smem[task, blk], lanes)
            picked = jnp.where(lane == row + half * HALF, jnp.broadcast_to(lanes, (HALF, 128)), 0.0)
            gates[n] = jnp.broadcast_to(jnp.sum(picked, axis=1, keepdims=True), (HALF, 128))

    def forward(k):
        four = pl.ds(k * CHUNK, CHUNK)
        span = pl.ds(pl.multiple_of((k % 2) * ROWS, ROWS), ROWS)
        gate = gates[four].reshape(ROWS, 128)
        for n in range(rows.shape[3] // 128):
            cols = pl.ds(n * 128, 128)
            cot = rows[four, 1, :, cols].reshape(ROWS, 128).astype(F32)
            sc[span, cols] = (gate * cot).astype(BF16)

        def body(n, _):
            cols = pl.ds(pl.multiple_of(n * NT, NT), NT)
            pre = jnp.dot(rows[four, 0].reshape(ROWS, rows.shape[3]), w1[:, cols], preferred_element_type=F32)
            back = jnp.dot(sc[span, :], w2t[:, cols], preferred_element_type=F32)
            sig = 0.5 * jnp.tanh(0.5 * pre) + 0.5
            value = pre * sig
            act[span, cols] = value.astype(BF16)
            pg[span, cols] = (back * (sig + value * (1.0 - sig))).astype(BF16)
            return 0

        lax.fori_loop(0, w1.shape[1] // NT, body, 0)

    def row_grads(k, r):
        span = pl.ds(pl.multiple_of((k % 2) * ROWS, ROWS), ROWS)

        def body(n, _):
            cols = pl.ds(pl.multiple_of(n * NT, NT), NT)
            part = jnp.dot(pg[span, :], w1t[:, cols], preferred_element_type=F32)
            rgb[pl.ds(r * CHUNK, CHUNK), :, cols] = part.reshape(CHUNK, HALF, NT)
            return 0

        lax.fori_loop(0, w1t.shape[1] // NT, body, 0)

    def turn(k):
        eight = pl.ds((k - 1) * CHUNK, 2 * CHUNK)
        width = xt.shape[0]
        for n in range(width // 256):
            cols = pl.ds(pl.multiple_of(yhi * width + n * 256, 256), 256)
            xt[pl.ds(n * 256, 256), :] = rows[eight, 0, :, cols].reshape(PAIR, 256).T
        width = actt.shape[0]
        for n in range(width // 256):
            cols = pl.ds(pl.multiple_of(yhi * width + n * 256, 256), 256)
            actt[pl.ds(n * 256, 256), :] = act[:, cols].T

    def grads():
        def body_in(n, _):
            cols = pl.ds(pl.multiple_of(n * NT, NT), NT)
            gin[:, cols] += jnp.dot(xt[...], pg[:, cols], preferred_element_type=F32)
            return 0

        def body_out(n, _):
            cols = pl.ds(pl.multiple_of(n * 256, 256), 256)
            gout[:, cols] += jnp.dot(actt[...], sc[:, cols], preferred_element_type=F32)
            return 0

        lax.fori_loop(0, gin.shape[1] // NT, body_in, 0)
        lax.fori_loop(0, gout.shape[1] // 256, body_out, 0)

    def last_grads():
        def body_in(n, _):
            cols = pl.ds(pl.multiple_of(n * NT, NT), NT)
            gin[:, cols] = (gin[:, cols] + jnp.dot(xt[...], pg[:, cols], preferred_element_type=F32)) * grad_scale
            return 0

        def body_out(n, _):
            cols = pl.ds(pl.multiple_of(n * 256, 256), 256)
            gout[:, cols] = (gout[:, cols] + jnp.dot(actt[...], sc[:, cols], preferred_element_type=F32)) * grad_scale
            return 0

        lax.fori_loop(0, gin.shape[1] // NT, body_in, 0)
        lax.fori_loop(0, gout.shape[1] // 256, body_out, 0)

    for copy in line_copies(0, 0):
        copy.start()
    for n in range(2):
        weight_copy(n).start()

    barrier = pltpu.get_barrier_semaphore()
    around = [(dy, dz) for dy in range(RING) for dz in range(RING) if dy or dz]
    for step in STEPS:
        pl.semaphore_signal(barrier, inc=1, device_id=on_line(*step), device_id_type=MESH)
    for step in around:
        pl.semaphore_signal(barrier, inc=1, device_id=on_plane(*step), device_id_type=MESH)
    make_tags()
    pl.semaphore_wait(barrier, LINE - 1 + RING * RING - 1)

    for step in STEPS:
        tag_line_copy(*step).start()
    for step in STEPS:
        for copy in line_copies(*step):
            copy.start()

    send_piece(0)
    send_piece(1)
    for n in range(1, LINE):
        arrive(tag_line.at[n], tagp_sem.at[n])
    tags = tag_line[0]
    for n in range(1, LINE):
        tags = tags + tag_line[n]
    tag_all[0] = tags
    for step in around:
        tag_copy(*step).start()
    for n in range(2, LINE):
        send_piece(n)

    gin[...] = jnp.zeros_like(gin)
    gout[...] = jnp.zeros_like(gout)
    for n in range(2):
        weight_copy(n).wait()
    transpose_weights()
    others = tag_all.at[pl.ds(1, RING * RING - 1)]
    arrive(others, tag_sem)
    make_gates()

    def step(k, _):
        @pl.when(k == 0)
        def _():
            wait_slots((A, 0, 1), (A, 0, 3), (A, 1, 0), (A, 3, 0))
            send_hops("z4", "y3")

        @pl.when(k == 1)
        def _():
            wait_slots((B, 0, 1), (B, 0, 3), (B, 3, 0), (B, 1, 0))
            send_hops("y4", "z3", "y5", "z5")

        @pl.when(k == 2)
        def _():
            wait_slots((A, 1, 1), (A, 1, 3), (B, 0, 2))
            send_hops("y6", "y7", "z6", "z7")
            wait_slots((B, 3, 1), (B, 1, 1), (A, 2, 0))
            send_hops("z8")

        @pl.when(k == 3)
        def _():
            wait_slots((A, 0, 2), (A, 1, 2), (B, 3, 3), (B, 3, 2))

        @pl.when(k == 6)
        def _():
            for half, dz in ((A, 1), (B, 3)):
                arrive(zq.at[half], zq_sem.at[half])
                zs[half, 1 if dz == 1 else 2] = (total(half, dz) + zq[half].astype(F32)).astype(BF16)
            z_copy(A, 1).start()
            z_copy(B, 3).start()
            wait_slots((B, 2, 0), (B, 2, 1))

        @pl.when(k == 7)
        def _():
            wait_slots((A, 3, 2), (A, 2, 2), (B, 2, 3), (B, 2, 2))

        forward(k)

        @pl.when(k < OWED)
        def _():
            row_grads(k, k)

        @pl.when(k == 2)
        def _():
            y_send((A, 1), (A, 3), (B, 1))

        @pl.when(k == 3)
        def _():
            y_send((A, 2), (B, 2), (B, 3), (A, 0), (B, 0))
            wait_slots((B, 1, 3), (B, 1, 2))
            send_hops("y8", "y9", "y10")

        @pl.when(k == 4)
        def _():
            for half, dz in ((A, 3), (B, 1)):
                zs[half, 1 if dz == 1 else 2] = total(half, dz).astype(BF16)
            z_copy(A, 3).start()
            z_copy(B, 1).start()
            wait_slots((A, 3, 1), (A, 3, 3))
            send_hops("z9")

        @pl.when(k == 5)
        def _():
            for half in (A, B):
                zs[half, 0] = total(half, 2).astype(BF16)
            for half in (A, B):
                relay_copy(half).start()
            wait_slots((A, 2, 1), (A, 2, 3))
            send_hops("z10")

        @pl.when(k == 6)
        def _():
            for half in (A, B):
                value = total(half, 0)
                for n in range(2):
                    arrive(zr.at[half, n], zr_sem.at[half, n])
                    value = value + zr[half, n].astype(F32)
                fs[pl.ds(half * HALF, HALF), :] = value.astype(BF16)
            for dr, dq in STEPS:
                home_copy(dr, dq).start()
            home[cap_rows(me), :] = fs[pl.ds(0, CAP), :]

        @pl.when(k % 2 == 1)
        def _():
            turn(k)

            @pl.when(k < 7)
            def _():
                grads()

            @pl.when(k == 7)
            def _():
                last_grads()

        return 0

    lax.fori_loop(0, len(ORDER) // CHUNK, step, 0)

    for dr, dq in STEPS:
        arrive(home.at[cap_rows(line_index(dr, dq))], home_sem.at[place(dr, dq)])
    home_ref[...] = home[...]

    for dr, dq in STEPS:
        tag_line_copy(dr, dq).wait_send()
        for copy in line_copies(dr, dq):
            copy.wait_send()
        home_copy(dr, dq).wait_send()
    arrive(others, tag_send)
    for name in HOPS:
        for n in range(2):
            hop_copy(name, n).wait_send()
    for half in (A, B):
        for dz in range(RING):
            y_copy(half, dz).wait_send()
        relay_copy(half).wait_send()
        for dz in (1, 3):
            z_copy(half, dz).wait_send()


def write_out(home_ref, gin_ref, gout_ref, home_hbm, gin_hbm, gout_hbm, home32, sem):
    copies = [pltpu.make_async_copy(gin_ref, gin_hbm, sem.at[0]), pltpu.make_async_copy(gout_ref, gout_hbm, sem.at[1])]
    for copy in copies:
        copy.start()
    home32[...] = home_ref[...].astype(F32)
    copies.append(pltpu.make_async_copy(home32, home_hbm, sem.at[2]))
    copies[2].start()
    for copy in copies:
        copy.wait()


def on_device(inputs, cotangent, task_ids, group_counts, task_gate, w_in, w_out):
    rows, width = inputs.shape
    hidden = w_in.shape[2]
    any_space = pl.BlockSpec(memory_space=pl.ANY)
    hbm = pl.BlockSpec(memory_space=pltpu.HBM)
    smem = pl.BlockSpec(memory_space=pltpu.SMEM)
    vmem = pl.BlockSpec(memory_space=pltpu.VMEM)
    dma = pltpu.SemaphoreType.DMA
    home, gin, gout = pl.pallas_call(
        kernel,
        out_shape=(
            jax.ShapeDtypeStruct((rows, width), BF16),
            jax.ShapeDtypeStruct((width // 2, hidden), F32),
            jax.ShapeDtypeStruct((hidden // 2, width), F32),
        ),
        in_specs=[hbm, hbm, vmem, smem, smem, hbm, hbm],
        out_specs=(vmem,) * 3,
        scratch_shapes=[
            pltpu.VMEM((len(ORDER), 2, HALF, width), BF16),
            pltpu.VMEM((width, hidden), BF16),
            pltpu.VMEM((hidden, width), BF16),
            pltpu.VMEM((hidden, width), BF16),
            pltpu.VMEM((width, hidden), BF16),
            pltpu.VMEM((PAIR, width), BF16),
            pltpu.VMEM((PAIR, hidden), BF16),
            pltpu.VMEM((PAIR, hidden), BF16),
            pltpu.VMEM((width // 2, PAIR), BF16),
            pltpu.VMEM((hidden // 2, PAIR), BF16),
            pltpu.VMEM((len(ORDER), HALF, 128), F32),
            pltpu.VMEM((LINE, 8, LINE * CAP), F32),
            pltpu.VMEM((LINE, 8, LINE * CAP), F32),
            pltpu.VMEM((RING * RING, 8, LINE * CAP), F32),
            pltpu.VMEM((OWED * CHUNK, HALF, width), F32),
            pltpu.VMEM((2, RING, HALF, width), BF16),
            pltpu.VMEM((2, RING, HALF, width), BF16),
            pltpu.VMEM((2, 3, HALF, width), BF16),
            pltpu.VMEM((2, HALF, width), BF16),
            pltpu.VMEM((2, 2, HALF, width), BF16),
            pltpu.VMEM((2 * HALF, width), BF16),
            pltpu.VMEM((2 * HALF, width), BF16),
            dma((2,)),
            dma((LINE,)),
            dma((LINE,)),
            dma((LINE,)),
            dma((LINE, 2)),
            dma(()),
            dma(()),
            dma((len(ORDER),)),
            dma((2 * len(HOPS),)),
            dma((2, RING)),
            dma((2, RING)),
            dma((2,)),
            dma((2,)),
            dma((2, 2)),
            dma((2, 2)),
            dma((LINE,)),
            dma((LINE,)),
        ],
        compiler_params=pltpu.CompilerParams(
            collective_id=0, has_side_effects=True, vmem_limit_bytes=VMEM_LIMIT
        ),
    )(inputs, cotangent, task_ids.reshape(1, rows), group_counts, task_gate, w_in[0], w_out[0])
    home, gin, gout = pl.pallas_call(
        write_out,
        out_shape=(
            jax.ShapeDtypeStruct((rows, width), F32),
            jax.ShapeDtypeStruct((width // 2, hidden), F32),
            jax.ShapeDtypeStruct((hidden // 2, width), F32),
        ),
        in_specs=[vmem, any_space, any_space],
        out_specs=(any_space,) * 3,
        scratch_shapes=[pltpu.VMEM((rows, width), F32), dma((3,))],
        compiler_params=pltpu.CompilerParams(vmem_limit_bytes=4 * 1024 * 1024),
    )(home, gin, gout)
    return home, gin[None], gout[None]


def solution(mesh):
    in_specs = (
        P(("blk", "dp"), None),
        P(("blk", "dp"), None),
        P(("blk", "dp")),
        P(("blk", "dp"), None),
        P(),
        P("blk", None, None),
        P("blk", None, None),
    )
    out_specs = (P(("blk", "dp"), None), P("blk", "dp", None), P("blk", "dp", None))
    return jax.shard_map(on_device, mesh=mesh, in_specs=in_specs, out_specs=out_specs, check_vma=False)
```

time: 108 us -> 94.5 us (0.88)
  Pallas kernels: 95 us -> 87.4 us
  local copies, waits for them, and re-layouts: 10.2 us -> 6.06 us
  other arithmetic: 2.06 us -> 0 us
    pallas_call x1 -> x2, Pallas kernels: 95 us -> 87.4 us  [the longest x1 83.9 us: on_device(): pl.pallas_call(kernel, out_shape=(jax.ShapeDtypeStruct((rows, width), BF1...]
    unnamed x5 -> x12, local copies, waits for them, and re-layouts: 8.75 us -> 6.06 us
    reduce_sum x1 -> x0, other arithmetic: 1.31 us -> none  [on_device(): jnp.sum(jnp.where(match[None, :], task_gate, 0.0), axis=1).reshape(1, tasks)]
where the time goes in v3:
time: 94.5 us; the launch traced here: 94.1 us
  Pallas kernels  87.4 us (92%)
  local copies, waits for them, and re-layouts  6.06 us (6%)
    pallas_call x1, Pallas kernels, on_device(): pl.pallas_call(kernel, out_shape=(jax.ShapeDtypeStruct((rows, width), BF1...  83.9 us
    unnamed x12, local copies, waits for them, and re-layouts  6.06 us
    pallas_call x1, Pallas kernels, on_device(): pl.pallas_call(write_out, out_shape=(jax.ShapeDtypeStruct((rows, width),...  3.46 us

profile of v3, /device:TPU:1, one launch (start us, length us, event | category | flops | bytes accessed | tf_op | source)
XLA Modules:
  0.0 94.1 jit_solution(5496689570407217380)
XLA Ops:
  0.6 0.0 copy-start.1
  0.6 0.9 copy-done.1
  1.6 0.0 copy-start.2
  1.6 0.9 %copy-done.2 = bf16[128,1024]{1,0:T(8,128)(2,1)S(1)} copy-done((bf16[128,1024]{1,0:T(8,128)(2,1)S(1)}, bf16[128,1024]{1,0:T(8,128)(2,1)}, u32[]{:S(2)}) %copy-start.2) | copy-done | bytes 262168
  2.5 0.0 copy-start.3
  2.5 0.7 copy-done.3
  3.2 0.0 copy-start.4
  3.2 0.7 copy-done.4
  3.9 0.0 copy-start.5
  3.9 0.7 copy-done.5
  4.5 83.9 %shard_map.94 = (bf16[128,1024]{1,0:T(8,128)(2,1)S(1)}, f32[512,2048]{1,0:T(8,128)S(1)}, f32[1024,1024]{1,0:T(8,128)}) custom-call(bf16[128,1024]{1,0:T(8,128)(2,1)S(1)} %copy-done.1, bf16[128,1024]{1,0:T(8,128)(2,1)S(1)} %copy-done.2, s32[1,128]{1,0:T(1,128)S(1)} %bitcast.5, s32[1,8]{1,0:T(1,128)S(1)} %copy-done.5, f32[4,64]{1,0:T(4,128)S(1)} %copy-done.3, ...), custom_call_target="tpu_custom_call" | custom-call | tf_op jit(solution)/shard_map/pallas_call | solution.py:484
  88.5 0.0 copy-start
  88.5 2.2 %copy-done = f32[1024,1024]{1,0:T(8,128)S(1)} copy-done((f32[1024,1024]{1,0:T(8,128)S(1)}, f32[1024,1024]{1,0:T(8,128)}, u32[]{:S(2)}) %copy-start) | copy-done | bytes 4194328
  90.7 3.5 %shard_map.95 = (f32[128,1024]{1,0:T(8,128)}, f32[512,2048]{1,0:T(8,128)}, f32[1024,1024]{1,0:T(8,128)}) custom-call(bf16[128,1024]{1,0:T(8,128)(2,1)S(1)} %get-tuple-element.9.home_ref, f32[512,2048]{1,0:T(8,128)S(1)} %get-tuple-element.10.gin_ref, f32[1024,1024]{1,0:T(8,128)S(1)} %copy-done), custom_call_target="tpu_custom_call" | custom-call | tf_op jit(solution)/shard_map/pallas_call | solution.py:538
Async XLA Ops:
  0.6 1.0 %copy-start.1 = (bf16[128,1024]{1,0:T(8,128)(2,1)S(1)}, bf16[128,1024]{1,0:T(8,128)(2,1)}, u32[]{:S(2)}) copy-start(bf16[128,1024]{1,0:T(8,128)(2,1)} %x_hbm.1) | copy-start | bytes 786436
  1.6 0.9 %copy-start.2 = (bf16[128,1024]{1,0:T(8,128)(2,1)S(1)}, bf16[128,1024]{1,0:T(8,128)(2,1)}, u32[]{:S(2)}) copy-start(bf16[128,1024]{1,0:T(8,128)(2,1)} %cot_hbm.1) | copy-start | bytes 786436
  2.5 0.7 copy-start.3
  3.2 0.7 copy-start.4
  3.9 0.7 copy-start.5
  88.5 2.2 %copy-start = (f32[1024,1024]{1,0:T(8,128)S(1)}, f32[1024,1024]{1,0:T(8,128)}, u32[]{:S(2)}) copy-start(f32[1024,1024]{1,0:T(8,128)} %get-tuple-element.11.gout_ref) | copy-start | bytes 12582916

commit v4 on v3

--- a/solution.py
+++ b/solution.py
@@ -17,7 +17,10 @@
 CHUNK = 4
 ROWS = CHUNK * HALF
 PAIR = 2 * ROWS
-NT = 512
+NT = 1024
+RT = 512
+GT_IN = 1024
+GT_OUT = 512
 VMEM_LIMIT = 46 * 1024 * 1024
 
 A, B = 0, 1
@@ -40,6 +43,10 @@
 
 
 STEPS = ((0, 1), (1, 0), (3, 0), (1, 1), (3, 1), (2, 0), (2, 1))
+
+
+def dot_t(left, right):
+    return lax.dot_general(left, right, (((1,), (1,)), ((), ())), preferred_element_type=F32)
 
 
 def hops():
@@ -86,10 +93,10 @@
 
 
 def kernel(
-    x_hbm, cot_hbm, ids_ref, count_smem, gate_smem, w1_hbm, w2_hbm,
+    x_hbm, cot_hbm, ids_hbm, count_smem, gate_smem, w1_hbm, w2_hbm,
     home_ref, gin, gout,
-    rows, w1, w2, w1t, w2t, sc, act, pg, xt, actt, gates, tag_out, tag_line, tag_all,
-    rgb, ys, ry, zs, zq, zr, fs, home,
+    rows, w1, w2, sc, act, pg, xt, actt, gates, tag_out, tag_line, tag_all,
+    rgb, ys, ry, zs, zq, zr, fs, home, ids_ref,
     local_sem, tagp_sem, tagp_send, line_sem, line_send, tag_sem, tag_send, slot_sem, hop_send,
     ry_sem, ry_send, zq_sem, zq_send, zr_sem, zr_send, home_sem, home_send,
 ):
@@ -198,15 +205,6 @@
     def total(half, dz):
         arrive(ry.at[half, dz], ry_sem.at[half, dz])
         return rgb[SLOT[(half, 0, dz)]] + ry[half, dz].astype(F32)
-
-    def transpose_weights():
-        def body(i, _):
-            cols = pl.ds(pl.multiple_of(i * 256, 256), 256)
-            w2t[:, cols] = w2[cols, :].T
-            w1t[cols, :] = w1[:, cols].T
-            return 0
-
-        lax.fori_loop(0, w1.shape[1] // 256, body, 0)
 
     def make_tags():
         lane = lax.broadcasted_iota(jnp.int32, (8, 128), 1)
@@ -243,7 +241,7 @@
         def body(n, _):
             cols = pl.ds(pl.multiple_of(n * NT, NT), NT)
             pre = jnp.dot(rows[four, 0].reshape(ROWS, rows.shape[3]), w1[:, cols], preferred_element_type=F32)
-            back = jnp.dot(sc[span, :], w2t[:, cols], preferred_element_type=F32)
+            back = dot_t(sc[span, :], w2[cols, :])
             sig = 0.5 * jnp.tanh(0.5 * pre) + 0.5
             value = pre * sig
             act[span, cols] = value.astype(BF16)
@@ -256,52 +254,45 @@
         span = pl.ds(pl.multiple_of((k % 2) * ROWS, ROWS), ROWS)
 
         def body(n, _):
-            cols = pl.ds(pl.multiple_of(n * NT, NT), NT)
-            part = jnp.dot(pg[span, :], w1t[:, cols], preferred_element_type=F32)
-            rgb[pl.ds(r * CHUNK, CHUNK), :, cols] = part.reshape(CHUNK, HALF, NT)
+            cols = pl.ds(pl.multiple_of(n * RT, RT), RT)
+            part = dot_t(pg[span, :], w1[cols, :])
+            rgb[pl.ds(r * CHUNK, CHUNK), :, cols] = part.reshape(CHUNK, HALF, RT)
             return 0
 
-        lax.fori_loop(0, w1t.shape[1] // NT, body, 0)
-
-    def turn(k):
-        eight = pl.ds((k - 1) * CHUNK, 2 * CHUNK)
+        lax.fori_loop(0, w1.shape[0] // RT, body, 0)
+
+    def turn(slots, first, count):
         width = xt.shape[0]
         for n in range(width // 256):
             cols = pl.ds(pl.multiple_of(yhi * width + n * 256, 256), 256)
-            xt[pl.ds(n * 256, 256), :] = rows[eight, 0, :, cols].reshape(PAIR, 256).T
+            xt[pl.ds(n * 256, 256), pl.ds(0, count)] = rows[slots, 0, :, cols].reshape(count, 256).T
         width = actt.shape[0]
         for n in range(width // 256):
             cols = pl.ds(pl.multiple_of(yhi * width + n * 256, 256), 256)
-            actt[pl.ds(n * 256, 256), :] = act[:, cols].T
-
-    def grads():
+            actt[pl.ds(n * 256, 256), pl.ds(0, count)] = act[pl.ds(first, count), cols].T
+
+    def grads(first, count, last=False):
+        here, span = pl.ds(0, count), pl.ds(first, count)
+
+        def add(acc, cols, value):
+            value = acc[:, cols] + value
+            acc[:, cols] = value * grad_scale if last else value
+
         def body_in(n, _):
-            cols = pl.ds(pl.multiple_of(n * NT, NT), NT)
-            gin[:, cols] += jnp.dot(xt[...], pg[:, cols], preferred_element_type=F32)
+            cols = pl.ds(pl.multiple_of(n * GT_IN, GT_IN), GT_IN)
+            add(gin, cols, jnp.dot(xt[:, here], pg[span, cols], preferred_element_type=F32))
             return 0
 
         def body_out(n, _):
-            cols = pl.ds(pl.multiple_of(n * 256, 256), 256)
-            gout[:, cols] += jnp.dot(actt[...], sc[:, cols], preferred_element_type=F32)
+            cols = pl.ds(pl.multiple_of(n * GT_OUT, GT_OUT), GT_OUT)
+            add(gout, cols, jnp.dot(actt[:, here], sc[span, cols], preferred_element_type=F32))
             return 0
 
-        lax.fori_loop(0, gin.shape[1] // NT, body_in, 0)
-        lax.fori_loop(0, gout.shape[1] // 256, body_out, 0)
-
-    def last_grads():
-        def body_in(n, _):
-            cols = pl.ds(pl.multiple_of(n * NT, NT), NT)
-            gin[:, cols] = (gin[:, cols] + jnp.dot(xt[...], pg[:, cols], preferred_element_type=F32)) * grad_scale
-            return 0
-
-        def body_out(n, _):
-            cols = pl.ds(pl.multiple_of(n * 256, 256), 256)
-            gout[:, cols] = (gout[:, cols] + jnp.dot(actt[...], sc[:, cols], preferred_element_type=F32)) * grad_scale
-            return 0
-
-        lax.fori_loop(0, gin.shape[1] // NT, body_in, 0)
-        lax.fori_loop(0, gout.shape[1] // 256, body_out, 0)
-
+        lax.fori_loop(0, gin.shape[1] // GT_IN, body_in, 0)
+        lax.fori_loop(0, gout.shape[1] // GT_OUT, body_out, 0)
+
+    ids_copy = pltpu.make_async_copy(ids_hbm, ids_ref, local_sem.at[2])
+    ids_copy.start()
     for copy in line_copies(0, 0):
         copy.start()
     for n in range(2):
@@ -313,6 +304,7 @@
         pl.semaphore_signal(barrier, inc=1, device_id=on_line(*step), device_id_type=MESH)
     for step in around:
         pl.semaphore_signal(barrier, inc=1, device_id=on_plane(*step), device_id_type=MESH)
+    ids_copy.wait()
     make_tags()
     pl.semaphore_wait(barrier, LINE - 1 + RING * RING - 1)
 
@@ -339,7 +331,6 @@
     gout[...] = jnp.zeros_like(gout)
     for n in range(2):
         weight_copy(n).wait()
-    transpose_weights()
     others = tag_all.at[pl.ds(1, RING * RING - 1)]
     arrive(others, tag_sem)
     make_gates()
@@ -358,7 +349,7 @@
         @pl.when(k == 2)
         def _():
             wait_slots((A, 1, 1), (A, 1, 3), (B, 0, 2))
-            send_hops("y6", "y7", "z6", "z7")
+            send_hops("y6", "z6", "z7")
             wait_slots((B, 3, 1), (B, 1, 1), (A, 2, 0))
             send_hops("z8")
 
@@ -387,33 +378,45 @@
 
         @pl.when(k == 2)
         def _():
-            y_send((A, 1), (A, 3), (B, 1))
+            y_send((A, 1), (B, 1))
+            send_hops("y7")
 
         @pl.when(k == 3)
         def _():
-            y_send((A, 2), (B, 2), (B, 3), (A, 0), (B, 0))
+            y_send((A, 2), (B, 2))
+            y_send((A, 3), (B, 3), (A, 0), (B, 0))
             wait_slots((B, 1, 3), (B, 1, 2))
             send_hops("y8", "y9", "y10")
+            wait_slots((A, 3, 1), (A, 3, 3))
+            send_hops("z9")
 
         @pl.when(k == 4)
         def _():
+            wait_slots((A, 2, 1), (A, 2, 3))
+            send_hops("z10")
+
+        @pl.when(k == 5)
+        def _():
+            for half in (A, B):
+                zs[half, 0] = total(half, 2).astype(BF16)
+            for half in (A, B):
+                relay_copy(half).start()
             for half, dz in ((A, 3), (B, 1)):
                 zs[half, 1 if dz == 1 else 2] = total(half, dz).astype(BF16)
             z_copy(A, 3).start()
             z_copy(B, 1).start()
-            wait_slots((A, 3, 1), (A, 3, 3))
-            send_hops("z9")
-
-        @pl.when(k == 5)
-        def _():
-            for half in (A, B):
-                zs[half, 0] = total(half, 2).astype(BF16)
-            for half in (A, B):
-                relay_copy(half).start()
-            wait_slots((A, 2, 1), (A, 2, 3))
-            send_hops("z10")
+
+        @pl.when((k % 2 == 1) & (k < 6))
+        def _():
+            turn(pl.ds((k - 1) * CHUNK, 2 * CHUNK), 0, PAIR)
+            grads(0, PAIR)
 
         @pl.when(k == 6)
+        def _():
+            turn(pl.ds(6 * CHUNK, CHUNK), 0, ROWS)
+            grads(0, ROWS)
+
+        @pl.when(k == 7)
         def _():
             for half in (A, B):
                 value = total(half, 0)
@@ -424,18 +427,8 @@
             for dr, dq in STEPS:
                 home_copy(dr, dq).start()
             home[cap_rows(me), :] = fs[pl.ds(0, CAP), :]
-
-        @pl.when(k % 2 == 1)
-        def _():
-            turn(k)
-
-            @pl.when(k < 7)
-            def _():
-                grads()
-
-            @pl.when(k == 7)
-            def _():
-                last_grads()
+            turn(pl.ds(7 * CHUNK, CHUNK), ROWS, ROWS)
+            grads(ROWS, ROWS, last=True)
 
         return 0
 
@@ -473,6 +466,10 @@
         copy.wait()
 
 
+def in_hbm(*arrays):
+    return tuple(pltpu.with_memory_space_constraint(array, pltpu.HBM) for array in arrays)
+
+
 def on_device(inputs, cotangent, task_ids, group_counts, task_gate, w_in, w_out):
     rows, width = inputs.shape
     hidden = w_in.shape[2]
@@ -484,18 +481,16 @@
     home, gin, gout = pl.pallas_call(
         kernel,
         out_shape=(
-            jax.ShapeDtypeStruct((rows, width), BF16),
-            jax.ShapeDtypeStruct((width // 2, hidden), F32),
-            jax.ShapeDtypeStruct((hidden // 2, width), F32),
+            pltpu.VMEM((rows, width), BF16),
+            pltpu.VMEM((width // 2, hidden), F32),
+            pltpu.VMEM((hidden // 2, width), F32),
         ),
-        in_specs=[hbm, hbm, vmem, smem, smem, hbm, hbm],
+        in_specs=[hbm, hbm, hbm, smem, smem, hbm, hbm],
         out_specs=(vmem,) * 3,
         scratch_shapes=[
             pltpu.VMEM((len(ORDER), 2, HALF, width), BF16),
             pltpu.VMEM((width, hidden), BF16),
             pltpu.VMEM((hidden, width), BF16),
-            pltpu.VMEM((hidden, width), BF16),
-            pltpu.VMEM((width, hidden), BF16),
             pltpu.VMEM((PAIR, width), BF16),
             pltpu.VMEM((PAIR, hidden), BF16),
             pltpu.VMEM((PAIR, hidden), BF16),
@@ -513,7 +508,8 @@
             pltpu.VMEM((2, 2, HALF, width), BF16),
             pltpu.VMEM((2 * HALF, width), BF16),
             pltpu.VMEM((2 * HALF, width), BF16),
-            dma((2,)),
+            pltpu.VMEM((1, 2 * HALF), jnp.int32),
+            dma((3,)),
             dma((LINE,)),
             dma((LINE,)),
             dma((LINE,)),
@@ -534,7 +530,7 @@
         compiler_params=pltpu.CompilerParams(
             collective_id=0, has_side_effects=True, vmem_limit_bytes=VMEM_LIMIT
         ),
-    )(inputs, cotangent, task_ids.reshape(1, rows), group_counts, task_gate, w_in[0], w_out[0])
+    )(*in_hbm(inputs, cotangent, task_ids.reshape(1, rows)), group_counts, task_gate, *in_hbm(w_in[0], w_out[0]))
     home, gin, gout = pl.pallas_call(
         write_out,
         out_shape=(

time: 94.5 us -> 83.4 us (0.88)
  local copies, waits for them, and re-layouts: 6.06 us -> 0 us
  Pallas kernels: 87.4 us -> 82.6 us
    unnamed x12 -> x0, local copies, waits for them, and re-layouts: 6.06 us -> none
    pallas_call x1, Pallas kernels: 83.9 us -> 79.1 us  [on_device(): pl.pallas_call(kernel, out_shape=(pltpu.VMEM((rows, width), BF16), pltpu....]
where the time goes in v4:
time: 83.4 us; the launch traced here: 83.2 us
  Pallas kernels  82.6 us (99%)
    pallas_call x1, Pallas kernels, on_device(): pl.pallas_call(kernel, out_shape=(pltpu.VMEM((rows, width), BF16), pltpu....  79.1 us
    pallas_call x1, Pallas kernels, on_device(): pl.pallas_call(write_out, out_shape=(jax.ShapeDtypeStruct((rows, width),...  3.46 us

profile of v4, /device:TPU:1, one launch (start us, length us, event | category | flops | bytes accessed | tf_op | source)
XLA Modules:
  0.0 83.2 jit_solution(14805626655503648663)
XLA Ops:
  0.6 79.1 %shard_map.94 = (bf16[128,1024]{1,0:T(8,128)(2,1)S(1)}, f32[512,2048]{1,0:T(8,128)S(1)}, f32[1024,1024]{1,0:T(8,128)S(1)}) custom-call(bf16[128,1024]{1,0:T(8,128)(2,1)} %x_hbm.1, bf16[128,1024]{1,0:T(8,128)(2,1)} %cot_hbm.1, s32[1,128]{1,0:T(1,128)} %bitcast.7, s32[1,8]{1,0:T(1,128)} %count_smem.1, f32[4,64]{1,0:T(4,128)} %gate_smem.1, ...), custom_call_target="tpu_custom_call" | custom-call | tf_op jit(solution)/shard_map/pallas_call | solution.py:481
  79.8 3.5 %shard_map.95 = (f32[128,1024]{1,0:T(8,128)}, f32[512,2048]{1,0:T(8,128)}, f32[1024,1024]{1,0:T(8,128)}) custom-call(bf16[128,1024]{1,0:T(8,128)(2,1)S(1)} %get-tuple-element.9.home_ref, f32[512,2048]{1,0:T(8,128)S(1)} %get-tuple-element.10.gin_ref, f32[1024,1024]{1,0:T(8,128)S(1)} %get-tuple-element.11.gout_ref), custom_call_target="tpu_custom_call" | custom-call | tf_op jit(solution)/shard_map/pallas_call | solution.py:534

commit v5 on v4

--- a/solution.py
+++ b/solution.py
@@ -28,14 +28,15 @@
     (A, 0, 0), (B, 0, 0), (A, 0, 1), (A, 0, 3),
     (A, 1, 0), (B, 0, 1), (B, 0, 3), (B, 3, 0),
     (A, 1, 1), (A, 1, 3), (B, 3, 1), (B, 0, 2),
+    (A, 3, 0), (B, 1, 0), (B, 1, 1), (B, 1, 3),
     (A, 0, 2), (A, 1, 2), (B, 3, 3), (B, 3, 2),
-    (A, 3, 0), (B, 1, 0), (B, 1, 1), (B, 1, 3),
     (A, 2, 0), (B, 1, 2), (A, 3, 1), (A, 3, 3),
-    (A, 2, 1), (A, 2, 3), (B, 2, 0), (B, 2, 1),
-    (A, 3, 2), (A, 2, 2), (B, 2, 3), (B, 2, 2),
+    (A, 2, 1), (A, 2, 3), (A, 3, 2), (B, 2, 0),
+    (A, 2, 2), (B, 2, 1), (B, 2, 3), (B, 2, 2),
 )
 SLOT = {key: n for n, key in enumerate(ORDER)}
-OWED = 4
+OWED = {0: 0, 1: 1, 2: 2, 4: 3}
+OWED_SLOT = {key: OWED[n // CHUNK] * CHUNK + n % CHUNK for key, n in SLOT.items() if n // CHUNK in OWED}
 
 
 def place(r, q):
@@ -185,7 +186,7 @@
 
     def y_send(*keys):
         for half, dz in keys:
-            ys[half, dz] = rgb[SLOT[(half, 1 if half == A else 3, dz)]].astype(BF16)
+            ys[half, dz] = rgb[OWED_SLOT[(half, 1 if half == A else 3, dz)]].astype(BF16)
         for half, dz in keys:
             y_copy(half, dz).start()
 
@@ -204,7 +205,7 @@
 
     def total(half, dz):
         arrive(ry.at[half, dz], ry_sem.at[half, dz])
-        return rgb[SLOT[(half, 0, dz)]] + ry[half, dz].astype(F32)
+        return rgb[OWED_SLOT[(half, 0, dz)]] + ry[half, dz].astype(F32)
 
     def make_tags():
         lane = lax.broadcasted_iota(jnp.int32, (8, 128), 1)
@@ -355,66 +356,17 @@
 
         @pl.when(k == 3)
         def _():
-            wait_slots((A, 0, 2), (A, 1, 2), (B, 3, 3), (B, 3, 2))
+            wait_slots((B, 1, 3))
+
+        @pl.when(k == 4)
+        def _():
+            wait_slots((A, 0, 2), (A, 1, 2), (A, 3, 1), (A, 3, 3))
+            send_hops("z9")
+            wait_slots((B, 3, 3), (B, 3, 2))
 
         @pl.when(k == 6)
         def _():
-            for half, dz in ((A, 1), (B, 3)):
-                arrive(zq.at[half], zq_sem.at[half])
-                zs[half, 1 if dz == 1 else 2] = (total(half, dz) + zq[half].astype(F32)).astype(BF16)
-            z_copy(A, 1).start()
-            z_copy(B, 3).start()
-            wait_slots((B, 2, 0), (B, 2, 1))
-
-        @pl.when(k == 7)
-        def _():
-            wait_slots((A, 3, 2), (A, 2, 2), (B, 2, 3), (B, 2, 2))
-
-        forward(k)
-
-        @pl.when(k < OWED)
-        def _():
-            row_grads(k, k)
-
-        @pl.when(k == 2)
-        def _():
-            y_send((A, 1), (B, 1))
-            send_hops("y7")
-
-        @pl.when(k == 3)
-        def _():
-            y_send((A, 2), (B, 2))
-            y_send((A, 3), (B, 3), (A, 0), (B, 0))
-            wait_slots((B, 1, 3), (B, 1, 2))
-            send_hops("y8", "y9", "y10")
-            wait_slots((A, 3, 1), (A, 3, 3))
-            send_hops("z9")
-
-        @pl.when(k == 4)
-        def _():
-            wait_slots((A, 2, 1), (A, 2, 3))
-            send_hops("z10")
-
-        @pl.when(k == 5)
-        def _():
-            for half in (A, B):
-                zs[half, 0] = total(half, 2).astype(BF16)
-            for half in (A, B):
-                relay_copy(half).start()
-            for half, dz in ((A, 3), (B, 1)):
-                zs[half, 1 if dz == 1 else 2] = total(half, dz).astype(BF16)
-            z_copy(A, 3).start()
-            z_copy(B, 1).start()
-
-        @pl.when((k % 2 == 1) & (k < 6))
-        def _():
-            turn(pl.ds((k - 1) * CHUNK, 2 * CHUNK), 0, PAIR)
-            grads(0, PAIR)
-
-        @pl.when(k == 6)
-        def _():
-            turn(pl.ds(6 * CHUNK, CHUNK), 0, ROWS)
-            grads(0, ROWS)
+            wait_slots((A, 3, 2), (B, 2, 0))
 
         @pl.when(k == 7)
         def _():
@@ -427,6 +379,62 @@
             for dr, dq in STEPS:
                 home_copy(dr, dq).start()
             home[cap_rows(me), :] = fs[pl.ds(0, CAP), :]
+            wait_slots((A, 2, 2), (B, 2, 1), (B, 2, 3), (B, 2, 2))
+
+        forward(k)
+
+        @pl.when((k < 3) | (k == 4))
+        def _():
+            row_grads(k, k - k // 4)
+
+        @pl.when(k == 2)
+        def _():
+            y_send((A, 1), (B, 1))
+            send_hops("y7")
+
+        @pl.when(k == 4)
+        def _():
+            y_send((A, 2), (B, 2))
+            y_send((A, 3), (B, 3), (A, 0), (B, 0))
+            wait_slots((B, 1, 2))
+            send_hops("y8", "y9", "y10")
+
+        @pl.when(k == 5)
+        def _():
+            wait_slots((A, 2, 1), (A, 2, 3))
+            send_hops("z10")
+
+        @pl.when(k == 6)
+        def _():
+            for half, dz in ((A, 3), (B, 1)):
+                zs[half, 1 if dz == 1 else 2] = total(half, dz).astype(BF16)
+            z_copy(A, 3).start()
+            z_copy(B, 1).start()
+
+        @pl.when((k % 2 == 1) & (k < 6))
+        def _():
+            turn(pl.ds((k - 1) * CHUNK, 2 * CHUNK), 0, PAIR)
+            grads(0, PAIR)
+
+        @pl.when(k == 5)
+        def _():
+            for half in (A, B):
+                zs[half, 0] = total(half, 2).astype(BF16)
+            for half in (A, B):
+                relay_copy(half).start()
+
+        @pl.when(k == 6)
+        def _():
+            turn(pl.ds(6 * CHUNK, CHUNK), 0, ROWS)
+            grads(0, ROWS)
+            for half, dz in ((A, 1), (B, 3)):
+                arrive(zq.at[half], zq_sem.at[half])
+                zs[half, 1 if dz == 1 else 2] = (total(half, dz) + zq[half].astype(F32)).astype(BF16)
+            z_copy(A, 1).start()
+            z_copy(B, 3).start()
+
+        @pl.when(k == 7)
+        def _():
             turn(pl.ds(7 * CHUNK, CHUNK), ROWS, ROWS)
             grads(ROWS, ROWS, last=True)
 
@@ -500,7 +508,7 @@
             pltpu.VMEM((LINE, 8, LINE * CAP), F32),
             pltpu.VMEM((LINE, 8, LINE * CAP), F32),
             pltpu.VMEM((RING * RING, 8, LINE * CAP), F32),
-            pltpu.VMEM((OWED * CHUNK, HALF, width), F32),
+            pltpu.VMEM((len(OWED) * CHUNK, HALF, width), F32),
             pltpu.VMEM((2, RING, HALF, width), BF16),
             pltpu.VMEM((2, RING, HALF, width), BF16),
             pltpu.VMEM((2, 3, HALF, width), BF16),

time: 83.4 us -> 79 us (0.947)
  Pallas kernels: 82.6 us -> 77.8 us
    pallas_call x1, Pallas kernels: 79.1 us -> 74.3 us  [on_device(): pl.pallas_call(kernel, out_shape=(pltpu.VMEM((rows, width), BF16), pltpu....]
where the time goes in v5:
time: 79 us; the launch traced here: 78.4 us
  Pallas kernels  77.8 us (98%)
    pallas_call x1, Pallas kernels, on_device(): pl.pallas_call(kernel, out_shape=(pltpu.VMEM((rows, width), BF16), pltpu....  74.3 us
    pallas_call x1, Pallas kernels, on_device(): pl.pallas_call(write_out, out_shape=(jax.ShapeDtypeStruct((rows, width),...  3.46 us

profile of v5, /device:TPU:1, one launch (start us, length us, event | category | flops | bytes accessed | tf_op | source)
XLA Modules:
  0.0 78.4 jit_solution(3643620290233925575)
XLA Ops:
  0.6 74.3 %shard_map.94 = (bf16[128,1024]{1,0:T(8,128)(2,1)S(1)}, f32[512,2048]{1,0:T(8,128)S(1)}, f32[1024,1024]{1,0:T(8,128)S(1)}) custom-call(bf16[128,1024]{1,0:T(8,128)(2,1)} %x_hbm.1, bf16[128,1024]{1,0:T(8,128)(2,1)} %cot_hbm.1, s32[1,128]{1,0:T(1,128)} %bitcast.7, s32[1,8]{1,0:T(1,128)} %count_smem.1, f32[4,64]{1,0:T(4,128)} %gate_smem.1, ...), custom_call_target="tpu_custom_call" | custom-call | tf_op jit(solution)/shard_map/pallas_call | solution.py:489
  75.0 3.5 %shard_map.95 = (f32[128,1024]{1,0:T(8,128)}, f32[512,2048]{1,0:T(8,128)}, f32[1024,1024]{1,0:T(8,128)}) custom-call(bf16[128,1024]{1,0:T(8,128)(2,1)S(1)} %get-tuple-element.9.home_ref, f32[512,2048]{1,0:T(8,128)S(1)} %get-tuple-element.10.gin_ref, f32[1024,1024]{1,0:T(8,128)S(1)} %get-tuple-element.11.gout_ref), custom_call_target="tpu_custom_call" | custom-call | tf_op jit(solution)/shard_map/pallas_call | solution.py:542

commit v6 on v5

--- a/solution.py
+++ b/solution.py
@@ -17,10 +17,10 @@
 CHUNK = 4
 ROWS = CHUNK * HALF
 PAIR = 2 * ROWS
-NT = 1024
-RT = 512
-GT_IN = 1024
-GT_OUT = 512
+NT = 2048
+RT = 1024
+GT_IN = 2048
+GT_OUT = 1024
 VMEM_LIMIT = 46 * 1024 * 1024
 
 A, B = 0, 1
@@ -52,40 +52,36 @@
 
 def hops():
     table = {}
-
-    def add(name, axis, half, dy, dz, split):
-        for sign in (1, -1):
-            if split:
-                if axis == "y":
-                    dy_s, dz_s = (-sign * dy) % RING, dz
-                else:
-                    dy_s, dz_s = dy, (-sign * dz) % RING
-                part = 0 if sign == 1 else 1
-            else:
-                dy_s, dz_s, part = dy, dz, None
+    both = ((0, PART), (PART, PART))
+
+    def add(name, axis, half, dy, dz, spans=(None, None)):
+        for sign, span in zip((1, -1), spans):
+            dy_s, dz_s = dy, dz
+            if spans[0] is not None and spans[0] != spans[1]:
+                dy_s, dz_s = ((-sign * dy) % RING, dz) if axis == "y" else (dy, (-sign * dz) % RING)
             there = (half, (dy_s - sign) % RING, dz_s) if axis == "y" else (half, dy_s, (dz_s - sign) % RING)
-            table.setdefault(name, []).append((axis, sign, (half, dy_s, dz_s), part, there))
-
-    add("y1", "y", A, 0, 0, False)
-    add("y2", "y", B, 0, 0, False)
-    add("y3", "y", A, 1, 0, True)
-    add("y4", "y", B, 0, 1, False)
-    add("y5", "y", B, 0, 3, False)
-    add("y6", "y", B, 0, 2, False)
-    add("y7", "y", B, 1, 0, True)
-    add("y8", "y", B, 1, 1, True)
-    add("y9", "y", B, 1, 3, True)
-    add("y10", "y", B, 1, 2, True)
-    add("z1", "z", B, 0, 0, False)
-    add("z2", "z", A, 0, 0, False)
-    add("z3", "z", B, 0, 1, True)
-    add("z4", "z", A, 1, 0, False)
-    add("z7", "z", A, 3, 0, False)
-    add("z5", "z", A, 0, 1, True)
-    add("z6", "z", A, 1, 1, True)
-    add("z8", "z", A, 2, 0, False)
-    add("z9", "z", A, 3, 1, True)
-    add("z10", "z", A, 2, 1, True)
+            table.setdefault(name, []).append((axis, sign, (half, dy_s, dz_s), span, there))
+
+    add("y1", "y", A, 0, 0)
+    add("y2", "y", B, 0, 0)
+    add("y3", "y", A, 1, 0, both)
+    add("y4", "y", B, 0, 1)
+    add("y5", "y", B, 0, 3)
+    add("y6", "y", B, 0, 2)
+    add("y7", "y", B, 1, 0, both)
+    add("y8", "y", B, 1, 1, both)
+    add("y9", "y", B, 1, 3, both)
+    add("y10", "y", B, 1, 2, both)
+    add("z1", "z", B, 0, 0)
+    add("z2", "z", A, 0, 0)
+    add("z3", "z", B, 0, 1, both)
+    add("z4", "z", A, 1, 0)
+    add("z5", "z", A, 0, 1, both)
+    add("z6", "z", A, 1, 1, both)
+    add("z7", "z", A, 3, 0)
+    add("z8", "z", A, 2, 0)
+    add("z9", "z", A, 3, 1, both)
+    add("z10", "z", A, 2, 1, both)
     return table
 
 
@@ -97,7 +93,7 @@
     x_hbm, cot_hbm, ids_hbm, count_smem, gate_smem, w1_hbm, w2_hbm,
     home_ref, gin, gout,
     rows, w1, w2, sc, act, pg, xt, actt, gates, tag_out, tag_line, tag_all,
-    rgb, ys, ry, zs, zq, zr, fs, home, ids_ref,
+    rgb, ys, ry, zs, zq, zr, fs, home, ids_ref, staged,
     local_sem, tagp_sem, tagp_send, line_sem, line_send, tag_sem, tag_send, slot_sem, hop_send,
     ry_sem, ry_send, zq_sem, zq_send, zr_sem, zr_send, home_sem, home_send,
 ):
@@ -144,20 +140,28 @@
                 yield pltpu.make_async_copy(src.at[here], rows.at[slot, kind, span], line_sem.at[there])
             else:
                 send = line_send.at[there, kind]
-                yield remote(src.at[here], rows.at[slot, kind, span], line_sem.at[there], send, on_line(dr, dq))
+                yield remote(staged.at[kind, here], rows.at[slot, kind, span], line_sem.at[there], send, on_line(dr, dq))
 
     def tag_line_copy(dr, dq):
         there = place((-dr) % RING, dq)
         return remote(tag_out.at[there], tag_line.at[there], tagp_sem.at[there], tagp_send.at[there], on_line(dr, dq))
 
-    def tag_copy(dy, dz):
-        there = ((-dy) % RING) * RING + (-dz) % RING
-        return remote(tag_all.at[0], tag_all.at[there], tag_sem, tag_send, on_plane(dy, dz))
+    def tag_y_copy(dy):
+        there = (-dy) % RING
+        return remote(tag_all.at[0], tag_all.at[there], tag_sem.at[0, there], tag_send.at[0, dy], on_plane(dy, 0))
+
+    def tag_z_copy(dz):
+        there = (-dz) % RING
+        src, dst = tag_all.at[pl.ds(0, RING)], tag_all.at[pl.ds(there * RING, RING)]
+        return remote(src, dst, tag_sem.at[1, there], tag_send.at[1, dz], on_plane(0, dz))
+
+    def stage_copy(n):
+        return pltpu.make_async_copy((x_hbm, cot_hbm)[n], staged.at[n], local_sem.at[3 + n])
 
     def hop_copy(name, n, span=None):
         axis, sign, here, part, there = HOPS[name][n]
         if part is not None:
-            span = pl.ds(part * PART, PART)
+            span = pl.ds(*part)
         src, dst = rows.at[SLOT[here]], rows.at[SLOT[there]]
         if span is not None:
             src, dst = rows.at[SLOT[here], :, span], rows.at[SLOT[there], :, span]
@@ -219,11 +223,12 @@
             moved = jnp.where(lane // CAP == n, pltpu.roll(tags, shift, 1), 0.0)
             (tag_line if n == 0 else tag_out)[n] = moved
 
-    def make_gates():
+    def make_gates(slots):
         row = lax.broadcasted_iota(jnp.int32, (HALF, 128), 0)
         lane = lax.broadcasted_iota(jnp.int32, (HALF, 128), 1)
-        for n, (half, dy, dz) in enumerate(ORDER):
-            tags = tag_all[dy * RING + dz][0:1, :]
+        for n in slots:
+            half, dy, dz = ORDER[n]
+            tags = tag_all[dz * RING + dy][0:1, :]
             lanes = jnp.zeros_like(tags)
             for task in range(4):
                 lanes = jnp.where(tags == float(task), gate_smem[task, blk], lanes)
@@ -297,17 +302,21 @@
     for copy in line_copies(0, 0):
         copy.start()
     for n in range(2):
+        stage_copy(n).start()
+    for n in range(2):
         weight_copy(n).start()
 
     barrier = pltpu.get_barrier_semaphore()
-    around = [(dy, dz) for dy in range(RING) for dz in range(RING) if dy or dz]
+    around = [(n, 0) for n in range(1, RING)] + [(0, n) for n in range(1, RING)]
     for step in STEPS:
         pl.semaphore_signal(barrier, inc=1, device_id=on_line(*step), device_id_type=MESH)
     for step in around:
         pl.semaphore_signal(barrier, inc=1, device_id=on_plane(*step), device_id_type=MESH)
     ids_copy.wait()
     make_tags()
-    pl.semaphore_wait(barrier, LINE - 1 + RING * RING - 1)
+    for n in range(2):
+        stage_copy(n).wait()
+    pl.semaphore_wait(barrier, len(STEPS) + len(around))
 
     for step in STEPS:
         tag_line_copy(*step).start()
@@ -323,18 +332,24 @@
     for n in range(1, LINE):
         tags = tags + tag_line[n]
     tag_all[0] = tags
-    for step in around:
-        tag_copy(*step).start()
-    for n in range(2, LINE):
+    for n in range(1, RING):
+        tag_y_copy(n).start()
+    for n in (2, 4):
+        send_piece(n)
+    for n in range(1, RING):
+        arrive(tag_all.at[n], tag_sem.at[0, n])
+    for n in range(1, RING):
+        tag_z_copy(n).start()
+    for n in (3, 5, 6, 7):
         send_piece(n)
 
     gin[...] = jnp.zeros_like(gin)
     gout[...] = jnp.zeros_like(gout)
     for n in range(2):
         weight_copy(n).wait()
-    others = tag_all.at[pl.ds(1, RING * RING - 1)]
-    arrive(others, tag_sem)
-    make_gates()
+    for n in range(1, RING):
+        arrive(tag_all.at[pl.ds(n * RING, RING)], tag_sem.at[1, n])
+    make_gates(range(CHUNK))
 
     def step(k, _):
         @pl.when(k == 0)
@@ -344,6 +359,7 @@
 
         @pl.when(k == 1)
         def _():
+            make_gates(range(CHUNK, len(ORDER)))
             wait_slots((B, 0, 1), (B, 0, 3), (B, 3, 0), (B, 1, 0))
             send_hops("y4", "z3", "y5", "z5")
 
@@ -451,7 +467,9 @@
         for copy in line_copies(dr, dq):
             copy.wait_send()
         home_copy(dr, dq).wait_send()
-    arrive(others, tag_send)
+    for n in range(1, RING):
+        tag_y_copy(n).wait_send()
+        tag_z_copy(n).wait_send()
     for name in HOPS:
         for n in range(2):
             hop_copy(name, n).wait_send()
@@ -517,13 +535,14 @@
             pltpu.VMEM((2 * HALF, width), BF16),
             pltpu.VMEM((2 * HALF, width), BF16),
             pltpu.VMEM((1, 2 * HALF), jnp.int32),
-            dma((3,)),
+            pltpu.VMEM((2, rows, width), BF16),
+            dma((5,)),
             dma((LINE,)),
             dma((LINE,)),
             dma((LINE,)),
             dma((LINE, 2)),
-            dma(()),
-            dma(()),
+            dma((2, RING)),
+            dma((2, RING)),
             dma((len(ORDER),)),
             dma((2 * len(HOPS),)),
             dma((2, RING)),

time: 79 us -> 75.8 us (0.959)
  Pallas kernels: 77.8 us -> 75 us
    pallas_call x1, Pallas kernels: 74.3 us -> 71.6 us  [on_device(): pl.pallas_call(kernel, out_shape=(pltpu.VMEM((rows, width), BF16), pltpu....]
where the time goes in v6:
time: 75.8 us; the launch traced here: 75.7 us
  Pallas kernels  75 us (99%)
    pallas_call x1, Pallas kernels, on_device(): pl.pallas_call(kernel, out_shape=(pltpu.VMEM((rows, width), BF16), pltpu....  71.6 us
    pallas_call x1, Pallas kernels, on_device(): pl.pallas_call(write_out, out_shape=(jax.ShapeDtypeStruct((rows, width),...  3.46 us

profile of v6, /device:TPU:1, one launch (start us, length us, event | category | flops | bytes accessed | tf_op | source)
XLA Modules:
  0.0 75.7 jit_solution(6050225875508423074)
XLA Ops:
  0.6 71.6 %shard_map.94 = (bf16[128,1024]{1,0:T(8,128)(2,1)S(1)}, f32[512,2048]{1,0:T(8,128)S(1)}, f32[1024,1024]{1,0:T(8,128)S(1)}) custom-call(bf16[128,1024]{1,0:T(8,128)(2,1)} %x_hbm.1, bf16[128,1024]{1,0:T(8,128)(2,1)} %cot_hbm.1, s32[1,128]{1,0:T(1,128)} %bitcast.7, s32[1,8]{1,0:T(1,128)} %count_smem.1, f32[4,64]{1,0:T(4,128)} %gate_smem.1, ...), custom_call_target="tpu_custom_call" | custom-call | tf_op jit(solution)/shard_map/pallas_call | solution.py:507
  72.2 3.5 %shard_map.95 = (f32[128,1024]{1,0:T(8,128)}, f32[512,2048]{1,0:T(8,128)}, f32[1024,1024]{1,0:T(8,128)}) custom-call(bf16[128,1024]{1,0:T(8,128)(2,1)S(1)} %get-tuple-element.9.home_ref, f32[512,2048]{1,0:T(8,128)S(1)} %get-tuple-element.10.gin_ref, f32[1024,1024]{1,0:T(8,128)S(1)} %get-tuple-element.11.gout_ref), custom_call_target="tpu_custom_call" | custom-call | tf_op jit(solution)/shard_map/pallas_call | solution.py:561
